TPU v7x, 128 devices: a whole 4x4x4 slice. The times are simulated.
128 devices in a mesh: section: 4 (over y), mp: 32 (over x, z, core).
Axes of the slice: x: 4, y: 4, z: 4, core: 2. Of those that a mesh axis runs over, the one named last changes fastest.
Arguments:
- hidden_in: bfloat16 [1, 4, 64, 4096], P(None, 'section'), may hold values from -36 to 36
- attn_gain: bfloat16 [4, 4096], P('section'), may hold values from 0.5 to 2
- w_query: bfloat16 [4, 4096, 4096], P('section', None, 'mp'), may hold values from -0.75 to 0.75
- w_key: bfloat16 [4, 4096, 1024], P('section', None, 'mp'), may hold values from -0.0625 to 0.0625
- w_value: bfloat16 [4, 4096, 1024], P('section', None, 'mp'), may hold values from -0.09375 to 0.09375
- w_out: bfloat16 [4, 4096, 4096], P('section', 'mp'), may hold values from -0.09375 to 0.09375
- ffn_gain: bfloat16 [4, 4096], P('section'), may hold values from 0.5 to 2
- w_gate: bfloat16 [4, 4096, 16384], P('section', None, 'mp'), may hold values from -0.09375 to 0.09375
- w_up: bfloat16 [4, 4096, 16384], P('section', None, 'mp'), may hold values from -0.09375 to 0.09375
- w_down: bfloat16 [4, 16384, 4096], P('section', 'mp'), may hold values from -0.046875 to 0.046875
- ffn_blocks: int32 [4, 4], P(None, 'section'), may hold values from 1 to 112
- heads_on: int32 [4, 4], P(None, 'section'), may hold values from 1 to 32
Outputs:
- hidden_out: bfloat16 [1, 4, 64, 4096], P(None, 'section')
Inputs may be any that keep to these rules, and one draw needn't show every extreme that they name: `ffn_blocks`: hidden units below 128 times the entry are active. `heads_on`: query heads below the entry are active.
All inputs are finite; a program needn't handle non-finite values.
Results may differ from a plain program's by a relative error of at most 0.025.
Values may be sent and summed in bfloat16 or wider, within the bound.
A program may use at most 128 MiB of HBM per device.

v0:
```python
import jax
import jax.numpy as jnp
from jax import lax
from jax.sharding import PartitionSpec as P

HEADS = 32
KV_HEADS = 8
HD = 128
BLOCK = 128


ROPE_BASE = 500000.0
EPSILON = 1e-05


def rows_first(arrays, axis, dims):
    turned = [jnp.moveaxis(a, dim, 0) for a, dim in zip(arrays, dims)]
    widths = [t[0].size for t in turned]
    both = jnp.concatenate([t.reshape(-1, w) for t, w in zip(turned, widths)], axis=1)
    out = lax.all_gather(both, axis, axis=0, tiled=True)
    pieces = jnp.split(out, [sum(widths[:k]) for k in range(1, len(widths))], axis=1)
    return tuple(
        (
            jnp.moveaxis(b.reshape(-1, *t.shape[1:]), 0, dim)
            for b, t, dim in zip(pieces, turned, dims)
        )
    )


def laid_out(pieces, dim):
    pieces = jnp.moveaxis(pieces, 0, dim)
    dims = pieces.shape
    return pieces.reshape(*dims[:dim], dims[dim] * dims[dim + 1], *dims[dim + 2 :])


def sent_to_all(array, axis):
    copies = jnp.broadcast_to(array, (lax.axis_size(axis), *array.shape))
    return lax.all_to_all(copies, axis, split_axis=0, concat_axis=0, tiled=True)


def collect(array, axis, dim):
    return laid_out(sent_to_all(array, axis), dim)


def in_blocks(array, dim, peers):
    dims = array.shape
    pieces = array.reshape(*dims[:dim], peers, dims[dim] // peers, *dims[dim + 1 :])
    return jnp.moveaxis(pieces, dim, 0)


def summed_on_arrival(array, axis, dim):
    peers = lax.axis_size(axis)
    pieces = lax.all_to_all(in_blocks(array, dim, peers), axis, 0, 0, tiled=True)
    return jnp.sum(pieces.astype(jnp.float32), axis=0)


def passed_along(array, axis, by):
    peers = lax.axis_size(axis)
    return lax.ppermute(array, axis, [(i, (i + by) % peers) for i in range(peers)])


def rms_scale(values, gain_row):
    mean_sq = jnp.mean(values * values, axis=-1, keepdims=True)
    return values * lax.rsqrt(mean_sq + EPSILON) * gain_row.astype(jnp.float32)


def rotate(values):
    length = values.shape[0]
    half_dim = values.shape[-1] // 2
    frequency = ROPE_BASE ** (-(jnp.arange(half_dim, dtype=jnp.float32) / half_dim))
    angles = jnp.arange(length, dtype=jnp.float32)[:, None] * frequency[None, :]
    cosine_table = jnp.cos(angles)[:, None, :]
    sine_table = jnp.sin(angles)[:, None, :]
    front_half = values[..., :half_dim].astype(jnp.float32)
    back_half = values[..., half_dim:].astype(jnp.float32)
    return jnp.concatenate(
        [
            front_half * cosine_table - back_half * sine_table,
            front_half * sine_table + back_half * cosine_table,
        ],
        axis=-1,
    )


def attend_local(projected, query_width, key_width, active, first_head):
    length = projected.shape[0]
    heads_here = query_width // HD
    group_size = HEADS // KV_HEADS
    queries = rotate(projected[:, :query_width].reshape(length, heads_here, HD)).astype(
        jnp.bfloat16
    )
    key_local = projected[:, query_width : query_width + key_width].astype(jnp.bfloat16)
    value_local = projected[:, query_width + key_width :].astype(jnp.bfloat16)
    key_whole, value_whole = rows_first((key_local, value_local), "mp", (1, 1))
    key_heads = key_whole.reshape(length, HD, KV_HEADS).transpose(0, 2, 1)
    value_heads = value_whole.reshape(length, HD, KV_HEADS).transpose(0, 2, 1)
    kv_here = max(1, heads_here // group_size)
    repeat_count = heads_here // kv_here
    first_kv = first_head // group_size
    key_pick = lax.dynamic_slice_in_dim(key_heads, first_kv, kv_here, 1)
    value_pick = lax.dynamic_slice_in_dim(value_heads, first_kv, kv_here, 1)
    keys_rot = jnp.repeat(rotate(key_pick).astype(jnp.bfloat16), repeat_count, axis=1)
    values = jnp.repeat(value_pick, repeat_count, axis=1)
    scores = jnp.einsum(
        "qhd,khd->hqk", queries, keys_rot, preferred_element_type=jnp.float32
    ) * HD ** (-0.5)
    causal = jnp.arange(length)[:, None] >= jnp.arange(length)[None, :]
    scores = jnp.where(causal[None], scores, -jnp.inf)
    probabilities = jax.nn.softmax(scores, axis=-1).astype(jnp.bfloat16)
    context = jnp.einsum("hqk,khd->qhd", probabilities, values, preferred_element_type=jnp.float32)
    head_ids = first_head + jnp.arange(heads_here)
    context = jnp.where((head_ids < active)[None, :, None], context, 0.0).astype(jnp.bfloat16)
    return context.reshape(length, query_width)


def per_device(
    hidden_in,
    attn_gain,
    w_query,
    w_key,
    w_value,
    w_out,
    ffn_gain,
    w_gate,
    w_up,
    w_down,
    ffn_blocks,
    heads_on,
):
    section_count = lax.axis_size("section")
    section_index = lax.axis_index("section")
    model_count = lax.axis_size("mp")
    model_index = lax.axis_index("mp")
    micro_total = ffn_blocks.shape[0]
    per_section = hidden_in.shape[0]
    length = hidden_in.shape[2]
    model_width = hidden_in.shape[3]
    local_rows = length // model_count
    units_here = w_gate.shape[2]
    query_width = w_query.shape[2]
    key_width = w_key.shape[2]
    first_head = model_index * (query_width // HD)
    first_unit = model_index * units_here
    joined_qkv = [jnp.concatenate([w_query[0], w_key[0], w_value[0]], axis=1)]
    joined_pair = [jnp.concatenate([w_gate[0], w_up[0]], axis=1)]

    def gated(pre_act, block_count):
        gate_part = pre_act[:, :units_here]
        up_part = pre_act[:, units_here:]
        unit_ids = first_unit + jnp.arange(units_here)
        return jnp.where(
            (unit_ids < BLOCK * block_count)[None, :], jax.nn.silu(gate_part) * up_part, 0.0
        ).astype(jnp.bfloat16)

    def layer_rows(carried, layer_pos, active, block_count):
        residual = carried.astype(jnp.float32)
        normed = rms_scale(residual, attn_gain[layer_pos]).astype(jnp.bfloat16)
        projected = jnp.dot(
            collect(normed, "mp", 0), joined_qkv[layer_pos], preferred_element_type=jnp.float32
        )
        context = attend_local(projected, query_width, key_width, active, first_head)
        attended = residual + summed_on_arrival(
            jnp.dot(context, w_out[layer_pos], preferred_element_type=jnp.float32).astype(
                jnp.bfloat16
            ),
            "mp",
            0,
        )
        normed_ffn = rms_scale(attended, ffn_gain[layer_pos]).astype(jnp.bfloat16)
        hidden = gated(
            jnp.dot(
                collect(normed_ffn, "mp", 0),
                joined_pair[layer_pos],
                preferred_element_type=jnp.float32,
            ),
            block_count,
        )
        return (
            attended
            + summed_on_arrival(
                jnp.dot(hidden, w_down[layer_pos], preferred_element_type=jnp.float32).astype(
                    jnp.bfloat16
                ),
                "mp",
                0,
            )
        ).astype(jnp.bfloat16)

    def section_work(carried, moment, layer_fn):
        micro_index = jnp.clip(moment - section_index, 0, micro_total - 1)
        carried = layer_fn(carried, 0, heads_on[micro_index, 0], ffn_blocks[micro_index, 0])
        return carried

    def tick_step(moment, loop_carry):
        carried, slot_buffer = loop_carry
        cycle_index = moment // section_count
        incoming = lax.dynamic_index_in_dim(
            slot_buffer, jnp.minimum(cycle_index, per_section - 1), 0, keepdims=False
        )
        incoming = jnp.where(moment < micro_total, incoming, jnp.zeros_like(incoming))
        at_head = section_index == 0
        written = lax.dynamic_update_index_in_dim(
            slot_buffer, carried, jnp.maximum(cycle_index - 1, 0), 0
        )
        slot_buffer = jnp.where(at_head & (moment >= section_count), written, slot_buffer)
        carried = jnp.where(at_head, incoming, carried)
        carried = section_work(carried, moment, layer_rows)
        carried = passed_along(carried, "section", 1)
        slot_buffer = passed_along(slot_buffer, "section", -1)
        return (carried, slot_buffer)

    slot_start = hidden_in.reshape(per_section, length, model_width)
    slot_start = lax.dynamic_slice_in_dim(slot_start, model_index * local_rows, local_rows, 1)
    initial = jnp.zeros((local_rows, model_width), jnp.bfloat16)
    finished = lax.fori_loop(0, micro_total + section_count, tick_step, (initial, slot_start))
    result = finished[1]
    result = collect(result, "mp", 1)
    return result.reshape(hidden_in.shape)


def solution(mesh):
    return jax.shard_map(
        per_device,
        mesh=mesh,
        in_specs=(
            P(None, "section", None, None),
            P("section", None),
            P("section", None, "mp"),
            P("section", None, "mp"),
            P("section", None, "mp"),
            P("section", "mp", None),
            P("section", None),
            P("section", None, "mp"),
            P("section", None, "mp"),
            P("section", "mp", None),
            P(None, "section"),
            P(None, "section"),
        ),
        out_specs=P(None, "section", None, None),
        check_vma=False,
    )
```

profile of v0, /device:TPU:25, one launch (start us, length us, event | category | flops | bytes accessed | tf_op | source)
XLA Modules:
  0.0 906.2 jit_solution(10943014542577423044)
XLA Ops:
  15.2 873.7 %while.21 = (s32[]{:T(128)}, bf16[2,4096]{1,0:T(2,128)(2,1)S(1)}, bf16[1,2,4096]{2,1,0:T(2,128)(2,1)S(1)}, pred[]{:T(512)}, s32[]{:T(128)}, /*index=5*/s32[]{:T(...) while((s32[]{:T(128)}, bf16[2,4096]{1,0:T(2,128)(2,1)S(1)}, ...), condition=%wide.region_7.8_spmd, body=%wide.region_0.7_spmd.sunk | while | flops 977384448 | bytes 49139016 | solution.py:215
  39.8 22.9 %all_gather.11 = bf16[1024,128]{1,0:T(8,128)(2,1)S(1)} all-gather(bf16[32,128]{1,0:T(8,128)(2,1)S(1)} %pad_maximum_fusion.4), channel_id=1, replica_groups=mesh['section'=4,'mp'=32] {'mp'}, dimensions={0}, use_global_device_ids=true | all-gather | bytes 270336 | tf_op jit(solution)/shard_map/while/body/eval_jaxpr/all_gather | solution.py:20
  71.1 11.6 %all-to-all-done.1 = bf16[32,2,4096]{2,1,0:T(2,128)(2,1)S(1)} async-done(((bf16[32,2,4096]{2,1,0:T(2,128)(2,1)}), bf16[32,2,4096]{2,1,0:T(2,128)(2,1)S(1)}, u32[]{:S(2)}, u32[]{:S(2)}) %all-to-all-start.1) | async-done | bytes 524320 | tf_op jit(solution)/shard_map/while/body/eval_jaxpr/all_to_all | solution.py:53
  112.9 10.9 %all-to-all-done.3 = bf16[32,2,4096]{2,1,0:T(2,128)(2,1)S(1)} async-done(((bf16[32,2,4096]{2,1,0:T(2,128)(2,1)}), bf16[32,2,4096]{2,1,0:T(2,128)(2,1)S(1)}, u32[]{:S(2)}, u32[]{:S(2)}) %all-to-all-start.3) | async-done | bytes 524320 | tf_op jit(solution)/shard_map/while/body/eval_jaxpr/all_to_all | solution.py:53
  147.7 22.9 %all_gather.11 = bf16[1024,128]{1,0:T(8,128)(2,1)S(1)} all-gather(bf16[32,128]{1,0:T(8,128)(2,1)S(1)} %pad_maximum_fusion.4), channel_id=1, replica_groups=mesh['section'=4,'mp'=32] {'mp'}, dimensions={0}, use_global_device_ids=true | all-gather | bytes 270336 | tf_op jit(solution)/shard_map/while/body/eval_jaxpr/all_gather | solution.py:20
  179.0 11.6 %all-to-all-done.1 = bf16[32,2,4096]{2,1,0:T(2,128)(2,1)S(1)} async-done(((bf16[32,2,4096]{2,1,0:T(2,128)(2,1)}), bf16[32,2,4096]{2,1,0:T(2,128)(2,1)S(1)}, u32[]{:S(2)}, u32[]{:S(2)}) %all-to-all-start.1) | async-done | bytes 524320 | tf_op jit(solution)/shard_map/while/body/eval_jaxpr/all_to_all | solution.py:53
  255.6 22.9 %all_gather.11 = bf16[1024,128]{1,0:T(8,128)(2,1)S(1)} all-gather(bf16[32,128]{1,0:T(8,128)(2,1)S(1)} %pad_maximum_fusion.4), channel_id=1, replica_groups=mesh['section'=4,'mp'=32] {'mp'}, dimensions={0}, use_global_device_ids=true | all-gather | bytes 270336 | tf_op jit(solution)/shard_map/while/body/eval_jaxpr/all_gather | solution.py:20
  286.9 11.6 %all-to-all-done.1 = bf16[32,2,4096]{2,1,0:T(2,128)(2,1)S(1)} async-done(((bf16[32,2,4096]{2,1,0:T(2,128)(2,1)}), bf16[32,2,4096]{2,1,0:T(2,128)(2,1)S(1)}, u32[]{:S(2)}, u32[]{:S(2)}) %all-to-all-start.1) | async-done | bytes 524320 | tf_op jit(solution)/shard_map/while/body/eval_jaxpr/all_to_all | solution.py:53
  363.8 22.9 %all_gather.11 = bf16[1024,128]{1,0:T(8,128)(2,1)S(1)} all-gather(bf16[32,128]{1,0:T(8,128)(2,1)S(1)} %pad_maximum_fusion.4), channel_id=1, replica_groups=mesh['section'=4,'mp'=32] {'mp'}, dimensions={0}, use_global_device_ids=true | all-gather | bytes 270336 | tf_op jit(solution)/shard_map/while/body/eval_jaxpr/all_gather | solution.py:20
  395.1 11.6 %all-to-all-done.1 = bf16[32,2,4096]{2,1,0:T(2,128)(2,1)S(1)} async-done(((bf16[32,2,4096]{2,1,0:T(2,128)(2,1)}), bf16[32,2,4096]{2,1,0:T(2,128)(2,1)S(1)}, u32[]{:S(2)}, u32[]{:S(2)}) %all-to-all-start.1) | async-done | bytes 524320 | tf_op jit(solution)/shard_map/while/body/eval_jaxpr/all_to_all | solution.py:53
  436.6 11.3 %all-to-all-done.3 = bf16[32,2,4096]{2,1,0:T(2,128)(2,1)S(1)} async-done(((bf16[32,2,4096]{2,1,0:T(2,128)(2,1)}), bf16[32,2,4096]{2,1,0:T(2,128)(2,1)S(1)}, u32[]{:S(2)}, u32[]{:S(2)}) %all-to-all-start.3) | async-done | bytes 524320 | tf_op jit(solution)/shard_map/while/body/eval_jaxpr/all_to_all | solution.py:53
  472.9 22.9 %all_gather.11 = bf16[1024,128]{1,0:T(8,128)(2,1)S(1)} all-gather(bf16[32,128]{1,0:T(8,128)(2,1)S(1)} %pad_maximum_fusion.4), channel_id=1, replica_groups=mesh['section'=4,'mp'=32] {'mp'}, dimensions={0}, use_global_device_ids=true | all-gather | bytes 270336 | tf_op jit(solution)/shard_map/while/body/eval_jaxpr/all_gather | solution.py:20
  504.2 11.6 %all-to-all-done.1 = bf16[32,2,4096]{2,1,0:T(2,128)(2,1)S(1)} async-done(((bf16[32,2,4096]{2,1,0:T(2,128)(2,1)}), bf16[32,2,4096]{2,1,0:T(2,128)(2,1)S(1)}, u32[]{:S(2)}, u32[]{:S(2)}) %all-to-all-start.1) | async-done | bytes 524320 | tf_op jit(solution)/shard_map/while/body/eval_jaxpr/all_to_all | solution.py:53
  545.6 11.4 %all-to-all-done.3 = bf16[32,2,4096]{2,1,0:T(2,128)(2,1)S(1)} async-done(((bf16[32,2,4096]{2,1,0:T(2,128)(2,1)}), bf16[32,2,4096]{2,1,0:T(2,128)(2,1)S(1)}, u32[]{:S(2)}, u32[]{:S(2)}) %all-to-all-start.3) | async-done | bytes 524320 | tf_op jit(solution)/shard_map/while/body/eval_jaxpr/all_to_all | solution.py:53
  582.0 22.9 %all_gather.11 = bf16[1024,128]{1,0:T(8,128)(2,1)S(1)} all-gather(bf16[32,128]{1,0:T(8,128)(2,1)S(1)} %pad_maximum_fusion.4), channel_id=1, replica_groups=mesh['section'=4,'mp'=32] {'mp'}, dimensions={0}, use_global_device_ids=true | all-gather | bytes 270336 | tf_op jit(solution)/shard_map/while/body/eval_jaxpr/all_gather | solution.py:20
  613.3 11.6 %all-to-all-done.1 = bf16[32,2,4096]{2,1,0:T(2,128)(2,1)S(1)} async-done(((bf16[32,2,4096]{2,1,0:T(2,128)(2,1)}), bf16[32,2,4096]{2,1,0:T(2,128)(2,1)S(1)}, u32[]{:S(2)}, u32[]{:S(2)}) %all-to-all-start.1) | async-done | bytes 524320 | tf_op jit(solution)/shard_map/while/body/eval_jaxpr/all_to_all | solution.py:53
  654.7 11.4 %all-to-all-done.3 = bf16[32,2,4096]{2,1,0:T(2,128)(2,1)S(1)} async-done(((bf16[32,2,4096]{2,1,0:T(2,128)(2,1)}), bf16[32,2,4096]{2,1,0:T(2,128)(2,1)S(1)}, u32[]{:S(2)}, u32[]{:S(2)}) %all-to-all-start.3) | async-done | bytes 524320 | tf_op jit(solution)/shard_map/while/body/eval_jaxpr/all_to_all | solution.py:53
  691.2 22.9 %all_gather.11 = bf16[1024,128]{1,0:T(8,128)(2,1)S(1)} all-gather(bf16[32,128]{1,0:T(8,128)(2,1)S(1)} %pad_maximum_fusion.4), channel_id=1, replica_groups=mesh['section'=4,'mp'=32] {'mp'}, dimensions={0}, use_global_device_ids=true | all-gather | bytes 270336 | tf_op jit(solution)/shard_map/while/body/eval_jaxpr/all_gather | solution.py:20
  722.4 11.6 %all-to-all-done.1 = bf16[32,2,4096]{2,1,0:T(2,128)(2,1)S(1)} async-done(((bf16[32,2,4096]{2,1,0:T(2,128)(2,1)}), bf16[32,2,4096]{2,1,0:T(2,128)(2,1)S(1)}, u32[]{:S(2)}, u32[]{:S(2)}) %all-to-all-start.1) | async-done | bytes 524320 | tf_op jit(solution)/shard_map/while/body/eval_jaxpr/all_to_all | solution.py:53
  763.8 11.4 %all-to-all-done.3 = bf16[32,2,4096]{2,1,0:T(2,128)(2,1)S(1)} async-done(((bf16[32,2,4096]{2,1,0:T(2,128)(2,1)}), bf16[32,2,4096]{2,1,0:T(2,128)(2,1)S(1)}, u32[]{:S(2)}, u32[]{:S(2)}) %all-to-all-start.3) | async-done | bytes 524320 | tf_op jit(solution)/shard_map/while/body/eval_jaxpr/all_to_all | solution.py:53
  800.3 22.9 %all_gather.11 = bf16[1024,128]{1,0:T(8,128)(2,1)S(1)} all-gather(bf16[32,128]{1,0:T(8,128)(2,1)S(1)} %pad_maximum_fusion.4), channel_id=1, replica_groups=mesh['section'=4,'mp'=32] {'mp'}, dimensions={0}, use_global_device_ids=true | all-gather | bytes 270336 | tf_op jit(solution)/shard_map/while/body/eval_jaxpr/all_gather | solution.py:20
  831.5 11.6 %all-to-all-done.1 = bf16[32,2,4096]{2,1,0:T(2,128)(2,1)S(1)} async-done(((bf16[32,2,4096]{2,1,0:T(2,128)(2,1)}), bf16[32,2,4096]{2,1,0:T(2,128)(2,1)S(1)}, u32[]{:S(2)}, u32[]{:S(2)}) %all-to-all-start.1) | async-done | bytes 524320 | tf_op jit(solution)/shard_map/while/body/eval_jaxpr/all_to_all | solution.py:53
  872.9 11.4 %all-to-all-done.3 = bf16[32,2,4096]{2,1,0:T(2,128)(2,1)S(1)} async-done(((bf16[32,2,4096]{2,1,0:T(2,128)(2,1)}), bf16[32,2,4096]{2,1,0:T(2,128)(2,1)S(1)}, u32[]{:S(2)}, u32[]{:S(2)}) %all-to-all-start.3) | async-done | bytes 524320 | tf_op jit(solution)/shard_map/while/body/eval_jaxpr/all_to_all | solution.py:53
  889.4 15.9 %all_to_all.57 = bf16[32,1,2,4096]{3,2,1,0:T(2,128)(2,1)S(1)} all-to-all(bf16[32,1,2,4096]{3,2,1,0:T(2,128)(2,1)S(1)} %broadcast_in_dim.154), channel_id=1, replica_groups=mesh['section'=4,'mp'=32] {'mp'}, dimensions={0} | all-to-all | bytes 1048576 | tf_op jit(solution)/shard_map/all_to_all | solution.py:38
  (420 shorter events, 539.6 us)
Async XLA Ops:
  16.8 20.2 %all-to-all-start = ((bf16[32,2,4096]{2,1,0:T(2,128)(2,1)}), bf16[32,2,4096]{2,1,0:T(2,128)(2,1)S(1)}, u32[]{:S(2)}, u32[]{:S(2)}) async-start(bf16[32,2,4096]{2,1,0:T(2,128)(2,1)} %broadcast_in_dim.182), calls=%async_computation | async-start | bytes 1048576 | tf_op jit(solution)/shard_map/while/body/eval_jaxpr/all_to_all | solution.py:38
  66.5 16.1 %all-to-all-start.1 = ((bf16[32,2,4096]{2,1,0:T(2,128)(2,1)}), bf16[32,2,4096]{2,1,0:T(2,128)(2,1)S(1)}, u32[]{:S(2)}, u32[]{:S(2)}) async-start(bf16[32,2,4096]{2,1,0:T(2,128)(2,1)} %reshape.303), calls=%async_computation.1 | async-start | bytes 1048576 | tf_op jit(solution)/shard_map/while/body/eval_jaxpr/all_to_all | solution.py:53
  84.6 15.7 %all-to-all-start.2 = ((bf16[32,2,4096]{2,1,0:T(2,128)(2,1)}), bf16[32,2,4096]{2,1,0:T(2,128)(2,1)}, u32[]{:S(2)}, u32[]{:S(2)}) async-start(bf16[32,2,4096]{2,1,0:T(2,128)(2,1)} %broadcast_in_dim.183), calls=%async_computation.2 | async-start | bytes 1048576 | tf_op jit(solution)/shard_map/while/body/eval_jaxpr/all_to_all | solution.py:38
  128.5 16.4 %all-to-all-start = ((bf16[32,2,4096]{2,1,0:T(2,128)(2,1)}), bf16[32,2,4096]{2,1,0:T(2,128)(2,1)S(1)}, u32[]{:S(2)}, u32[]{:S(2)}) async-start(bf16[32,2,4096]{2,1,0:T(2,128)(2,1)} %broadcast_in_dim.182), calls=%async_computation | async-start | bytes 1048576 | tf_op jit(solution)/shard_map/while/body/eval_jaxpr/all_to_all | solution.py:38
  174.4 16.1 %all-to-all-start.1 = ((bf16[32,2,4096]{2,1,0:T(2,128)(2,1)}), bf16[32,2,4096]{2,1,0:T(2,128)(2,1)S(1)}, u32[]{:S(2)}, u32[]{:S(2)}) async-start(bf16[32,2,4096]{2,1,0:T(2,128)(2,1)} %reshape.303), calls=%async_computation.1 | async-start | bytes 1048576 | tf_op jit(solution)/shard_map/while/body/eval_jaxpr/all_to_all | solution.py:53
  192.5 15.7 %all-to-all-start.2 = ((bf16[32,2,4096]{2,1,0:T(2,128)(2,1)}), bf16[32,2,4096]{2,1,0:T(2,128)(2,1)}, u32[]{:S(2)}, u32[]{:S(2)}) async-start(bf16[32,2,4096]{2,1,0:T(2,128)(2,1)} %broadcast_in_dim.183), calls=%async_computation.2 | async-start | bytes 1048576 | tf_op jit(solution)/shard_map/while/body/eval_jaxpr/all_to_all | solution.py:38
  236.4 16.4 %all-to-all-start = ((bf16[32,2,4096]{2,1,0:T(2,128)(2,1)}), bf16[32,2,4096]{2,1,0:T(2,128)(2,1)S(1)}, u32[]{:S(2)}, u32[]{:S(2)}) async-start(bf16[32,2,4096]{2,1,0:T(2,128)(2,1)} %broadcast_in_dim.182), calls=%async_computation | async-start | bytes 1048576 | tf_op jit(solution)/shard_map/while/body/eval_jaxpr/all_to_all | solution.py:38
  282.3 16.1 %all-to-all-start.1 = ((bf16[32,2,4096]{2,1,0:T(2,128)(2,1)}), bf16[32,2,4096]{2,1,0:T(2,128)(2,1)S(1)}, u32[]{:S(2)}, u32[]{:S(2)}) async-start(bf16[32,2,4096]{2,1,0:T(2,128)(2,1)} %reshape.303), calls=%async_computation.1 | async-start | bytes 1048576 | tf_op jit(solution)/shard_map/while/body/eval_jaxpr/all_to_all | solution.py:53
  300.4 15.7 %all-to-all-start.2 = ((bf16[32,2,4096]{2,1,0:T(2,128)(2,1)}), bf16[32,2,4096]{2,1,0:T(2,128)(2,1)}, u32[]{:S(2)}, u32[]{:S(2)}) async-start(bf16[32,2,4096]{2,1,0:T(2,128)(2,1)} %broadcast_in_dim.183), calls=%async_computation.2 | async-start | bytes 1048576 | tf_op jit(solution)/shard_map/while/body/eval_jaxpr/all_to_all | solution.py:38
  344.9 16.1 %all-to-all-start = ((bf16[32,2,4096]{2,1,0:T(2,128)(2,1)}), bf16[32,2,4096]{2,1,0:T(2,128)(2,1)S(1)}, u32[]{:S(2)}, u32[]{:S(2)}) async-start(bf16[32,2,4096]{2,1,0:T(2,128)(2,1)} %broadcast_in_dim.182), calls=%async_computation | async-start | bytes 1048576 | tf_op jit(solution)/shard_map/while/body/eval_jaxpr/all_to_all | solution.py:38
  390.6 16.1 %all-to-all-start.1 = ((bf16[32,2,4096]{2,1,0:T(2,128)(2,1)}), bf16[32,2,4096]{2,1,0:T(2,128)(2,1)S(1)}, u32[]{:S(2)}, u32[]{:S(2)}) async-start(bf16[32,2,4096]{2,1,0:T(2,128)(2,1)} %reshape.303), calls=%async_computation.1 | async-start | bytes 1048576 | tf_op jit(solution)/shard_map/while/body/eval_jaxpr/all_to_all | solution.py:53
  408.6 15.7 %all-to-all-start.2 = ((bf16[32,2,4096]{2,1,0:T(2,128)(2,1)}), bf16[32,2,4096]{2,1,0:T(2,128)(2,1)}, u32[]{:S(2)}, u32[]{:S(2)}) async-start(bf16[32,2,4096]{2,1,0:T(2,128)(2,1)} %broadcast_in_dim.183), calls=%async_computation.2 | async-start | bytes 1048576 | tf_op jit(solution)/shard_map/while/body/eval_jaxpr/all_to_all | solution.py:38
  454.0 16.1 %all-to-all-start = ((bf16[32,2,4096]{2,1,0:T(2,128)(2,1)}), bf16[32,2,4096]{2,1,0:T(2,128)(2,1)S(1)}, u32[]{:S(2)}, u32[]{:S(2)}) async-start(bf16[32,2,4096]{2,1,0:T(2,128)(2,1)} %broadcast_in_dim.182), calls=%async_computation | async-start | bytes 1048576 | tf_op jit(solution)/shard_map/while/body/eval_jaxpr/all_to_all | solution.py:38
  499.7 16.1 %all-to-all-start.1 = ((bf16[32,2,4096]{2,1,0:T(2,128)(2,1)}), bf16[32,2,4096]{2,1,0:T(2,128)(2,1)S(1)}, u32[]{:S(2)}, u32[]{:S(2)}) async-start(bf16[32,2,4096]{2,1,0:T(2,128)(2,1)} %reshape.303), calls=%async_computation.1 | async-start | bytes 1048576 | tf_op jit(solution)/shard_map/while/body/eval_jaxpr/all_to_all | solution.py:53
  517.7 15.7 %all-to-all-start.2 = ((bf16[32,2,4096]{2,1,0:T(2,128)(2,1)}), bf16[32,2,4096]{2,1,0:T(2,128)(2,1)}, u32[]{:S(2)}, u32[]{:S(2)}) async-start(bf16[32,2,4096]{2,1,0:T(2,128)(2,1)} %broadcast_in_dim.183), calls=%async_computation.2 | async-start | bytes 1048576 | tf_op jit(solution)/shard_map/while/body/eval_jaxpr/all_to_all | solution.py:38
  563.1 16.1 %all-to-all-start = ((bf16[32,2,4096]{2,1,0:T(2,128)(2,1)}), bf16[32,2,4096]{2,1,0:T(2,128)(2,1)S(1)}, u32[]{:S(2)}, u32[]{:S(2)}) async-start(bf16[32,2,4096]{2,1,0:T(2,128)(2,1)} %broadcast_in_dim.182), calls=%async_computation | async-start | bytes 1048576 | tf_op jit(solution)/shard_map/while/body/eval_jaxpr/all_to_all | solution.py:38
  608.8 16.1 %all-to-all-start.1 = ((bf16[32,2,4096]{2,1,0:T(2,128)(2,1)}), bf16[32,2,4096]{2,1,0:T(2,128)(2,1)S(1)}, u32[]{:S(2)}, u32[]{:S(2)}) async-start(bf16[32,2,4096]{2,1,0:T(2,128)(2,1)} %reshape.303), calls=%async_computation.1 | async-start | bytes 1048576 | tf_op jit(solution)/shard_map/while/body/eval_jaxpr/all_to_all | solution.py:53
  626.9 15.7 %all-to-all-start.2 = ((bf16[32,2,4096]{2,1,0:T(2,128)(2,1)}), bf16[32,2,4096]{2,1,0:T(2,128)(2,1)}, u32[]{:S(2)}, u32[]{:S(2)}) async-start(bf16[32,2,4096]{2,1,0:T(2,128)(2,1)} %broadcast_in_dim.183), calls=%async_computation.2 | async-start | bytes 1048576 | tf_op jit(solution)/shard_map/while/body/eval_jaxpr/all_to_all | solution.py:38
  672.2 16.1 %all-to-all-start = ((bf16[32,2,4096]{2,1,0:T(2,128)(2,1)}), bf16[32,2,4096]{2,1,0:T(2,128)(2,1)S(1)}, u32[]{:S(2)}, u32[]{:S(2)}) async-start(bf16[32,2,4096]{2,1,0:T(2,128)(2,1)} %broadcast_in_dim.182), calls=%async_computation | async-start | bytes 1048576 | tf_op jit(solution)/shard_map/while/body/eval_jaxpr/all_to_all | solution.py:38
  717.9 16.1 %all-to-all-start.1 = ((bf16[32,2,4096]{2,1,0:T(2,128)(2,1)}), bf16[32,2,4096]{2,1,0:T(2,128)(2,1)S(1)}, u32[]{:S(2)}, u32[]{:S(2)}) async-start(bf16[32,2,4096]{2,1,0:T(2,128)(2,1)} %reshape.303), calls=%async_computation.1 | async-start | bytes 1048576 | tf_op jit(solution)/shard_map/while/body/eval_jaxpr/all_to_all | solution.py:53
  736.0 15.7 %all-to-all-start.2 = ((bf16[32,2,4096]{2,1,0:T(2,128)(2,1)}), bf16[32,2,4096]{2,1,0:T(2,128)(2,1)}, u32[]{:S(2)}, u32[]{:S(2)}) async-start(bf16[32,2,4096]{2,1,0:T(2,128)(2,1)} %broadcast_in_dim.183), calls=%async_computation.2 | async-start | bytes 1048576 | tf_op jit(solution)/shard_map/while/body/eval_jaxpr/all_to_all | solution.py:38
  781.3 16.1 %all-to-all-start = ((bf16[32,2,4096]{2,1,0:T(2,128)(2,1)}), bf16[32,2,4096]{2,1,0:T(2,128)(2,1)S(1)}, u32[]{:S(2)}, u32[]{:S(2)}) async-start(bf16[32,2,4096]{2,1,0:T(2,128)(2,1)} %broadcast_in_dim.182), calls=%async_computation | async-start | bytes 1048576 | tf_op jit(solution)/shard_map/while/body/eval_jaxpr/all_to_all | solution.py:38
  827.0 16.1 %all-to-all-start.1 = ((bf16[32,2,4096]{2,1,0:T(2,128)(2,1)}), bf16[32,2,4096]{2,1,0:T(2,128)(2,1)S(1)}, u32[]{:S(2)}, u32[]{:S(2)}) async-start(bf16[32,2,4096]{2,1,0:T(2,128)(2,1)} %reshape.303), calls=%async_computation.1 | async-start | bytes 1048576 | tf_op jit(solution)/shard_map/while/body/eval_jaxpr/all_to_all | solution.py:53
  845.1 15.7 %all-to-all-start.2 = ((bf16[32,2,4096]{2,1,0:T(2,128)(2,1)}), bf16[32,2,4096]{2,1,0:T(2,128)(2,1)}, u32[]{:S(2)}, u32[]{:S(2)}) async-start(bf16[32,2,4096]{2,1,0:T(2,128)(2,1)} %broadcast_in_dim.183), calls=%async_computation.2 | async-start | bytes 1048576 | tf_op jit(solution)/shard_map/while/body/eval_jaxpr/all_to_all | solution.py:38
  (37 other events, 322.5 us)
where the time goes:
time: 915 us; the launch traced here: 906 us
  waiting for transfers between devices  354 us (39%)
  blocking collectives  199 us (22%)
  starting transfers between devices  164 us (18%)
  matrix products  75 us (8%)
  local copies, waits for them, and re-layouts  73 us (8%)
  other arithmetic  34.3 us (4%)
    all_gather x8, blocking collectives, rows_first(): out = lax.all_gather(both, axis, axis=0, tiled=True)  184 us
    all_to_all x16, waiting for transfers between devices, summed_on_arrival(): lax.all_to_all(in_blocks(array, dim, peers), axis, 0, 0, tiled=True)  182 us
    all_to_all x16, waiting for transfers between devices, sent_to_all(): return lax.all_to_all(copies, axis, split_axis=0, concat_axis=0, tiled=True)  163 us
    all_to_all x16, starting transfers between devices, sent_to_all(): return lax.all_to_all(copies, axis, split_axis=0, concat_axis=0, tiled=True)  75.7 us
    all_to_all x16, starting transfers between devices, summed_on_arrival(): lax.all_to_all(in_blocks(array, dim, peers), axis, 0, 0, tiled=True)  65.6 us
    dot_general x8, matrix products, layer_rows(): jnp.dot(collect(normed_ffn, 'mp', 0), joined_pair[layer_pos], preferred_e...  40.8 us
    ppermute x16, starting transfers between devices, passed_along(): lax.ppermute(array, axis, [(i, (i + by) % peers) for i in range(peers)])  22.2 us
    broadcast_in_dim x17, local copies, waits for them, and re-layouts, sent_to_all(): copies = jnp.broadcast_to(array, (lax.axis_size(axis), *array.shape))  20.7 us
  transfers between devices with their start and end apart: 48, of which 40 were waited for; matrix products, arithmetic and copies ran while one was open for 2% of the time, Pallas kernels for 0%

commit v1 on v0

v1 whole, which is shorter than its diff:
```python
import functools

import jax
import jax.numpy as jnp
import numpy as np
from jax import lax
from jax.experimental import pallas as pl
from jax.experimental.pallas import tpu as pltpu
from jax.sharding import PartitionSpec as P

HEADS = 32
KV_HEADS = 8
HD = 128
BLOCK = 128
D = 4096
LEN = 64
N = 32
UNITS = 512
MICRO = 4
SECTIONS = 4
ROPE_BASE = 500000.0
EPSILON = 1e-05
MESH = pl.DeviceIdType.MESH
BF = jnp.bfloat16
F32 = jnp.float32
S_AG1, S_KV, S_RS1, S_AG2, S_RS2 = range(5)


def body(
    hid, again, wq, wk, wv, wo, fgain, wg, wu, wd, blocks, heads,
    cs, sn, cst, snt, pk, pv,
    out,
    x0, xa, xb, r1, r2, p1, p2, kvs, kvr, obuf, yb, att, xg, hbuf, qs,
    wqkv, wkb, wvb, wob, wgb, wub, wdb,
    send_sem, recv_sem, xin_sem, yh_sem, misc_sem, w_sem,
):
    sec = lax.axis_index("section")
    me = lax.axis_index("mp")
    head_id = me
    kv_id = me // (HEADS // KV_HEADS)

    def dev(s, d):
        return (s, d)

    def others(fn):
        def step(k, carry):
            fn(lax.rem(me + k, N))
            return carry

        lax.fori_loop(1, N, step, 0)

    loads = [
        (wq.at[0], wqkv.at[:, pl.ds(0, HD)]),
        (wk.at[0], wkb),
        (wv.at[0], wvb),
        (wo.at[0], wob),
        (wg.at[0], wgb),
        (wu.at[0], wub),
        (wd.at[0], wdb),
    ]
    weight = [pltpu.make_async_copy(s, d, w_sem.at[i]) for i, (s, d) in enumerate(loads)]

    def load_hidden(dst, sem):
        def step(j, carry):
            cols = pl.ds(pl.multiple_of(j * 128, 128), 128)
            pltpu.make_async_copy(hid.at[0, 0, :, cols], dst.at[j], sem).start()
            return carry

        lax.fori_loop(0, N, step, 0)

    @pl.when(sec == 0)
    def _():
        load_hidden(xa.at[0], xin_sem.at[0])

    @pl.when(sec != 0)
    def _():
        load_hidden(x0, misc_sem.at[0])

    for w in weight:
        w.start()

    barrier = pltpu.get_barrier_semaphore()

    def greet(d):
        pl.semaphore_signal(barrier, inc=1, device_id=dev(sec, d), device_id_type=MESH)

    others(greet)
    for k in range(1, SECTIONS):
        pl.semaphore_signal(
            barrier, inc=1, device_id=dev(lax.rem(sec + k, SECTIONS), me), device_id_type=MESH
        )

    weight[1].wait()
    weight[2].wait()

    def permute_rows(i, carry):
        rows = pl.ds(pl.multiple_of(i * 512, 512), 512)
        both = jnp.dot(wkb[rows, :], pk[...], preferred_element_type=F32) + jnp.dot(
            wvb[rows, :], pv[...], preferred_element_type=F32
        )
        wqkv[rows, pl.ds(HD, HD)] = both.astype(BF)
        return carry

    lax.fori_loop(0, D // 512, permute_rows, 0)

    pl.semaphore_wait(barrier, N - 1 + SECTIONS - 1)

    @pl.when(sec != 0)
    def _():
        pltpu.make_async_copy(x0, x0, misc_sem.at[0]).wait()
        pltpu.make_async_remote_copy(
            src_ref=x0, dst_ref=xa.at[sec], send_sem=misc_sem.at[1], recv_sem=xin_sem.at[sec],
            device_id=dev(0, me), device_id_type=MESH,
        ).start()

    weight[0].wait()

    def broadcast(src, dst, m, phase):
        def send(d):
            pltpu.make_async_remote_copy(
                src_ref=src, dst_ref=dst, send_sem=send_sem.at[phase, m],
                recv_sem=recv_sem.at[phase, m], device_id=dev(sec, d), device_id_type=MESH,
            ).start()

        others(send)

    def wait_recv(buf, phase, m):
        view = buf.at[m, pl.ds(0, N - 1)]
        pltpu.make_async_copy(view, view, recv_sem.at[phase, m]).wait()

    def wait_send(buf, phase, m):
        view = buf.at[m, pl.ds(0, N - 1)]
        pltpu.make_async_copy(view, view, send_sem.at[phase, m]).wait()

    def scaled(buf, m, gain):
        total = jnp.zeros((LEN, 128), F32)
        for j in range(N):
            value = buf[m, j].astype(F32)
            total = total + value * value
            cols = slice(j * 128, (j + 1) * 128)
            xg[:, cols] = (value * gain[:, cols].astype(F32)).astype(BF)
        mean_sq = jnp.sum(total, axis=-1, keepdims=True) * (1.0 / D)
        return lax.rsqrt(mean_sq + EPSILON)

    def total_of(buf, m):
        total = buf[m, 0].astype(F32)
        for j in range(1, N):
            total = total + buf[m, j].astype(F32)
        return total

    def project(m):
        @pl.when(sec == 0)
        def _():
            pltpu.make_async_copy(xa.at[m], xa.at[m], xin_sem.at[m]).wait()

        @pl.when(sec != 0)
        def _():
            pltpu.make_async_copy(yb.at[m], yb.at[m], yh_sem.at[m]).wait()
            broadcast(xa.at[m, me], xa.at[m, me], m, S_AG1)
            wait_recv(xa, S_AG1, m)

        scale = scaled(xa, m, again)
        qkv = jnp.dot(xg[...], wqkv[...], preferred_element_type=F32) * scale
        kv = qkv[:, HD : 2 * HD].astype(BF).astype(F32)
        turned = kv.T
        pairs = jnp.concatenate([turned[0:32, :], turned[32:64, :]], axis=1)
        kvs[m] = pairs.reshape(KV_HEADS, 4, 128)
        kvr[m, me] = kvs[m, kv_id]

        def send(d):
            pltpu.make_async_remote_copy(
                src_ref=kvs.at[m, d // (HEADS // KV_HEADS)], dst_ref=kvr.at[m, me],
                send_sem=send_sem.at[S_KV, m], recv_sem=recv_sem.at[S_KV, m],
                device_id=dev(sec, d), device_id_type=MESH,
            ).start()

        others(send)
        q = qkv[:, :HD]
        half = HD // 2
        swapped = jnp.concatenate([q[:, half:], q[:, :half]], axis=1)
        qs[m] = (q * cs[...] + swapped * sn[...]).astype(BF)

    def attend(m):
        wait_recv(kvr, S_KV, m)
        both = kvr[m].reshape(HD, 128)
        kt = both[:, :LEN]
        vt = both[:, LEN:].astype(BF)
        half = HD // 2
        u, v = kt[:half], kt[half:]
        keys = jnp.concatenate(
            [u * cst[...] - v * snt[...], u * snt[...] + v * cst[...]], axis=0
        ).astype(BF)
        scores = jnp.dot(qs[m], keys, preferred_element_type=F32) * HD ** (-0.5)
        row = lax.broadcasted_iota(jnp.int32, (LEN, LEN), 0)
        col = lax.broadcasted_iota(jnp.int32, (LEN, LEN), 1)
        scores = jnp.where(row >= col, scores, -jnp.inf)
        top = jnp.max(scores, axis=-1, keepdims=True)
        e = jnp.exp(scores - top)
        prob = (e / jnp.sum(e, axis=-1, keepdims=True)).astype(BF)
        context = lax.dot_general(
            prob, vt, (((1,), (1,)), ((), ())), preferred_element_type=F32
        )
        on = jnp.full((LEN, HD), heads[m, 0], jnp.int32) > head_id
        context = jnp.where(on, context, 0.0).astype(BF)

        def column(i, carry):
            cols = pl.ds(pl.multiple_of(i * 1024, 1024), 1024)
            term = jnp.dot(context, wob[:, cols], preferred_element_type=F32).astype(BF)
            for j in range(8):
                p1[m, i * 8 + j] = term[:, j * 128 : (j + 1) * 128]
            return carry

        lax.fori_loop(0, 4, column, 0)
        scatter(p1, r1, m, S_RS1)

    def scatter(src, dst, m, phase):
        def send(d):
            pltpu.make_async_remote_copy(
                src_ref=src.at[m, d], dst_ref=dst.at[m, me], send_sem=send_sem.at[phase, m],
                recv_sem=recv_sem.at[phase, m], device_id=dev(sec, d), device_id_type=MESH,
            ).start()

        others(send)
        dst[m, me] = src[m, me]

    def attended(m):
        wait_recv(r1, S_RS1, m)
        value = xa[m, me].astype(F32) + total_of(r1, m)
        att[m] = value
        xb[m, me] = value.astype(BF)
        broadcast(xb.at[m, me], xb.at[m, me], m, S_AG2)

    def feed(m):
        wait_recv(xb, S_AG2, m)
        scale = scaled(xb, m, fgain)
        limit = jnp.full((LEN, 256), blocks[m, 0], jnp.int32) * BLOCK

        def unit(i, carry):
            cols = pl.ds(pl.multiple_of(i * 256, 256), 256)
            gate = jnp.dot(xg[...], wgb[:, cols], preferred_element_type=F32) * scale
            up = jnp.dot(xg[...], wub[:, cols], preferred_element_type=F32) * scale
            ids = me * UNITS + i * 256 + lax.broadcasted_iota(jnp.int32, (LEN, 256), 1)
            value = gate / (1.0 + jnp.exp(-gate)) * up
            hbuf[:, cols] = jnp.where(ids < limit, value, 0.0).astype(BF)
            return carry

        lax.fori_loop(0, 2, unit, 0)

        def column(i, carry):
            cols = pl.ds(pl.multiple_of(i * 1024, 1024), 1024)
            term = jnp.dot(hbuf[...], wdb[:, cols], preferred_element_type=F32).astype(BF)
            for j in range(8):
                p2[m, i * 8 + j] = term[:, j * 128 : (j + 1) * 128]
            return carry

        lax.fori_loop(0, 4, column, 0)
        scatter(p2, r2, m, S_RS2)

    def finish(m):
        wait_recv(r2, S_RS2, m)
        yb[m] = (att[m] + total_of(r2, m)).astype(BF)

        @pl.when(sec < SECTIONS - 1)
        def _():
            pltpu.make_async_remote_copy(
                src_ref=yb.at[m], dst_ref=xa.at[m, me], send_sem=send_sem.at[5, m],
                recv_sem=yh_sem.at[m], device_id=dev(sec + 1, me), device_id_type=MESH,
            ).start()

        @pl.when((sec == SECTIONS - 1) & (m < MICRO - 1))
        def _():
            pltpu.make_async_remote_copy(
                src_ref=yb.at[m], dst_ref=obuf.at[me], send_sem=send_sem.at[5, m],
                recv_sem=misc_sem.at[2], device_id=dev(m, me), device_id_type=MESH,
            ).start()

    def micro(m, carry):
        @pl.when(m == 0)
        def _():
            weight[3].wait()

        project(m)
        attend(m)
        attended(m)

        @pl.when(m == 0)
        def _():
            for w in weight[4:]:
                w.wait()

        feed(m)
        finish(m)
        return carry

    lax.fori_loop(0, MICRO, micro, 0)

    @pl.when(sec == SECTIONS - 1)
    def _():
        obuf[me] = yb[MICRO - 1]

    @pl.when(sec != SECTIONS - 1)
    def _():
        pltpu.make_async_copy(yb.at[0], yb.at[0], misc_sem.at[2]).wait()

    def send_out(d):
        pltpu.make_async_remote_copy(
            src_ref=obuf.at[me], dst_ref=obuf.at[me], send_sem=misc_sem.at[3],
            recv_sem=misc_sem.at[4], device_id=dev(sec, d), device_id_type=MESH,
        ).start()

    others(send_out)
    view = obuf.at[pl.ds(0, N - 1)]
    pltpu.make_async_copy(view, view, misc_sem.at[4]).wait()
    done = pltpu.make_async_copy(obuf, out, misc_sem.at[5])
    done.start()

    def drain(m, carry):
        @pl.when(sec != 0)
        def _():
            wait_send(xa, S_AG1, m)

        wait_send(kvr, S_KV, m)
        wait_send(r1, S_RS1, m)
        wait_send(xb, S_AG2, m)
        wait_send(r2, S_RS2, m)

        @pl.when((sec < SECTIONS - 1) | (m < MICRO - 1))
        def _():
            pltpu.make_async_copy(yb.at[m], yb.at[m], send_sem.at[5, m]).wait()

        return carry

    lax.fori_loop(0, MICRO, drain, 0)

    @pl.when(sec != 0)
    def _():
        pltpu.make_async_copy(x0, x0, misc_sem.at[1]).wait()

    pltpu.make_async_copy(view, view, misc_sem.at[3]).wait()
    done.wait()


def tables():
    half = HD // 2
    frequency = ROPE_BASE ** (-(np.arange(half, dtype=np.float64) / half))
    angles = np.arange(LEN, dtype=np.float64)[:, None] * frequency[None, :]
    c, s = np.cos(angles).astype(np.float32), np.sin(angles).astype(np.float32)
    cs = np.concatenate([c, c], axis=1)
    sn = np.concatenate([-s, s], axis=1)
    pk = np.zeros((32, HD), np.float32)
    pv = np.zeros((32, HD), np.float32)
    for j in range(4):
        for k in range(KV_HEADS):
            pk[j * KV_HEADS + k, k * 4 + j] = 1.0
            pv[j * KV_HEADS + k, 32 + k * 4 + j] = 1.0
    return (
        jnp.asarray(cs), jnp.asarray(sn),
        jnp.asarray(np.ascontiguousarray(c.T)), jnp.asarray(np.ascontiguousarray(s.T)),
        jnp.asarray(pk, BF), jnp.asarray(pv, BF),
    )


def per_device(*args):
    any_spec = pl.BlockSpec(memory_space=pl.ANY)
    vmem = pl.BlockSpec(memory_space=pltpu.VMEM)
    smem = pl.BlockSpec(memory_space=pltpu.SMEM)
    piece = (LEN, 128)
    whole = (MICRO, N, *piece)
    gathered = pl.pallas_call(
        body,
        out_shape=jax.ShapeDtypeStruct((N, *piece), BF),
        in_specs=[
            any_spec, vmem, any_spec, any_spec, any_spec, any_spec, vmem, any_spec, any_spec,
            any_spec, smem, smem, vmem, vmem, vmem, vmem, vmem, vmem,
        ],
        out_specs=any_spec,
        scratch_shapes=[
            pltpu.VMEM((N, *piece), BF),
            pltpu.VMEM(whole, BF),
            pltpu.VMEM(whole, BF),
            pltpu.VMEM(whole, BF),
            pltpu.VMEM(whole, BF),
            pltpu.VMEM(whole, BF),
            pltpu.VMEM(whole, BF),
            pltpu.VMEM((MICRO, KV_HEADS, 4, 128), F32),
            pltpu.VMEM((MICRO, N, 4, 128), F32),
            pltpu.VMEM((N, *piece), BF),
            pltpu.VMEM((MICRO, *piece), BF),
            pltpu.VMEM((MICRO, *piece), F32),
            pltpu.VMEM((LEN, D), BF),
            pltpu.VMEM((LEN, UNITS), BF),
            pltpu.VMEM((MICRO, *piece), BF),
            pltpu.VMEM((D, 256), BF),
            pltpu.VMEM((D, 32), BF),
            pltpu.VMEM((D, 32), BF),
            pltpu.VMEM((HD, D), BF),
            pltpu.VMEM((D, UNITS), BF),
            pltpu.VMEM((D, UNITS), BF),
            pltpu.VMEM((UNITS, D), BF),
            pltpu.SemaphoreType.DMA((6, MICRO)),
            pltpu.SemaphoreType.DMA((5, MICRO)),
            pltpu.SemaphoreType.DMA((MICRO,)),
            pltpu.SemaphoreType.DMA((MICRO,)),
            pltpu.SemaphoreType.DMA((6,)),
            pltpu.SemaphoreType.DMA((7,)),
        ],
        compiler_params=pltpu.CompilerParams(
            collective_id=0, has_side_effects=True, vmem_limit_bytes=56 * 1024 * 1024
        ),
    )(*args, *tables())
    return gathered.transpose(1, 0, 2).reshape(1, 1, LEN, D)


def solution(mesh):
    return jax.shard_map(
        per_device,
        mesh=mesh,
        in_specs=(
            P(None, "section", None, None),
            P("section", None),
            P("section", None, "mp"),
            P("section", None, "mp"),
            P("section", None, "mp"),
            P("section", "mp", None),
            P("section", None),
            P("section", None, "mp"),
            P("section", None, "mp"),
            P("section", "mp", None),
            P(None, "section"),
            P(None, "section"),
        ),
        out_specs=P(None, "section", None, None),
        check_vma=False,
    )
```

time: 915 us -> 349 us (0.38)
  waiting for transfers between devices: 354 us -> 0 us
  Pallas kernels: 0 us -> 339 us
  blocking collectives: 199 us -> 0 us
  starting transfers between devices: 164 us -> 0 us
  matrix products: 75 us -> 0 us
  local copies, waits for them, and re-layouts: 73 us -> 9.64 us
  other arithmetic: 34.3 us -> 0 us
    all_to_all x32 -> x0, waiting for transfers between devices: 345 us -> none  [the longest x16 182 us: summed_on_arrival(): lax.all_to_all(in_blocks(array, dim, peers), axis, 0, 0, tiled=True)]
    pallas_call x0 -> x1, Pallas kernels: none -> 339 us  [per_device(): pl.pallas_call(body, out_shape=jax.ShapeDtypeStruct((N, *piece), BF), in_...]
    all_gather x8 -> x0, blocking collectives: 184 us -> none  [rows_first(): out = lax.all_gather(both, axis, axis=0, tiled=True)]
    all_to_all x32 -> x0, starting transfers between devices: 141 us -> none  [the longest x16 75.7 us: sent_to_all(): return lax.all_to_all(copies, axis, split_axis=0, concat_axis=0, tiled=True)]
    dot_general x40 -> x0, matrix products: 75 us -> none  [the longest x8 40.8 us: layer_rows(): jnp.dot(collect(normed_ffn, 'mp', 0), joined_pair[layer_pos], preferred_e...]
    reshape x48 -> x1, local copies, waits for them, and re-layouts: 37.1 us -> 1.02 us  [per_device(): return gathered.transpose(1, 0, 2).reshape(1, 1, LEN, D)]
    ppermute x16 -> x0, starting transfers between devices: 22.2 us -> none  [passed_along(): lax.ppermute(array, axis, [(i, (i + by) % peers) for i in range(peers)])]
    broadcast_in_dim x17 -> x0, local copies, waits for them, and re-layouts: 20.7 us -> none  [sent_to_all(): copies = jnp.broadcast_to(array, (lax.axis_size(axis), *array.shape))]
  transfers between devices with their start and end apart: 48 -> 0, of which waited for: 40 -> 0; matrix products, arithmetic and copies ran while one was open for 2% -> 0% of each run, Pallas kernels for 0% -> 0%
where the time goes in v1:
time: 349 us
  Pallas kernels  339 us (97%)
  local copies, waits for them, and re-layouts  9.64 us (3%)
    pallas_call x1, Pallas kernels, per_device(): pl.pallas_call(body, out_shape=jax.ShapeDtypeStruct((N, *piece), BF), in_...  339 us
    unnamed x4, local copies, waits for them, and re-layouts  7.23 us

profile of v1, /device:TPU:25, one launch (start us, length us, event | category | flops | bytes accessed | tf_op | source)
XLA Modules:
  0.0 348.9 jit_solution(17046321482973522142)
XLA Ops:
  0.0 1.3 copy.25.blocks
  1.3 1.3 copy.26.heads
  2.6 2.3 copy.23.wk
  4.9 2.3 copy.24.wv
  7.2 339.3 %shard_map.172 = bf16[32,64,128]{2,1,0:T(8,128)(2,1)} custom-call(bf16[1,1,64,4096]{3,2,1,0:T(8,128)(2,1)} %hid.1, bf16[1,4096]{1,0:T(2,128)(2,1)} %again.1, bf16[1,4096,128]{2,1,0:T(8,128)(2,1)} %wq.1, bf16[1,4096,32]{2,1,0:T(8,128)(2,1)} %copy.23.wk, bf16[1,4096,32]{2,1,0:T(8,128)(2,1)} %copy.24.wv, bf16[1,128,4096]{2,1,0:T(8,128)(2,1)} %wo.1, ...), custom_call_target="tpu_custom_call" | custom-call | tf_op jit(solution)/shard_map/pallas_call | solution.py:369
  346.5 1.4 copy.27
  347.9 1.0 reshape.3

commit v2 on v1

v2 whole, which is shorter than its diff:
```python
import functools

import jax
import jax.numpy as jnp
import numpy as np
from jax import lax
from jax.experimental import pallas as pl
from jax.experimental.pallas import tpu as pltpu
from jax.sharding import PartitionSpec as P

HEADS = 32
KV_HEADS = 8
HD = 128
BLOCK = 128
D = 4096
LEN = 64
N = 32
UNITS = 512
MICRO = 4
SECTIONS = 4
ROPE_BASE = 500000.0
EPSILON = 1e-05
MESH = pl.DeviceIdType.MESH
BF = jnp.bfloat16
F32 = jnp.float32
CHIPS = 16
(
    S_IN, S_Y, S_AG1, S_PASS1, S_KV, S_GIVE1, S_RS1, S_RS2, S_AG2, S_PASS2, S_GIVE2, S_AG3, S_PASS3,
) = range(13)
RING = (0, 1, 2, 1)
FAR_FIRST = sorted(
    [(dx, dz) for dx in range(4) for dz in range(4) if (dx, dz) != (0, 0)],
    key=lambda d: -(RING[d[0]] + RING[d[1]]),
)


def body(
    hid, again, wq, wk, wv, wo, fgain, wg, wu, wd, blocks, heads,
    cs, sn, cst, snt, pk, pv,
    out,
    x0, xa, xb, r1, r2, pt, ps, dr, own, kvs, kvr, obuf, yb, att, xg, acc, hbuf, qs,
    wqkv, wkb, wvb, wob, wgb, wub, wdb,
    send_sem, recv_sem, misc_sem, w_sem,
):
    sec = lax.axis_index("section")
    me = lax.axis_index("mp")
    chip = me // 2
    core = lax.rem(me, 2)
    rest = 1 - core
    partner = chip * 2 + rest
    mine = core * CHIPS + chip
    kv_id = me // (HEADS // KV_HEADS)
    at_x, at_z = chip // 4, lax.rem(chip, 4)

    def others(fn):
        for dx, dz in FAR_FIRST:
            fn(lax.rem(at_x + dx, 4) * 4 + lax.rem(at_z + dz, 4))

    def remote(src, dst, phase, m, s, d):
        return pltpu.make_async_remote_copy(
            src_ref=src, dst_ref=dst, send_sem=send_sem.at[phase, m],
            recv_sem=recv_sem.at[phase, m], device_id=(s, d), device_id_type=MESH,
        )

    def received(view, phase, m):
        pltpu.make_async_copy(view, view, recv_sem.at[phase, m]).wait()

    def sent(view, phase, m):
        pltpu.make_async_copy(view, view, send_sem.at[phase, m]).wait()

    def half(which):
        return pl.ds(pl.multiple_of(which * CHIPS, CHIPS), CHIPS)

    loads = [
        (wk.at[0], wkb),
        (wv.at[0], wvb),
        (wq.at[0], wqkv.at[:, pl.ds(0, HD)]),
        (wo.at[0], wob),
        (wg.at[0], wgb),
        (wu.at[0], wub),
        (wd.at[0], wdb),
    ]
    weight = [pltpu.make_async_copy(s, d, w_sem.at[i]) for i, (s, d) in enumerate(loads)]

    def load_hidden(dst, first, sem):
        def step(j, carry):
            cols = pl.ds(pl.multiple_of((core * CHIPS + j) * 128, 128), 128)
            pltpu.make_async_copy(hid.at[0, 0, :, cols], dst.at[first + j], sem).start()
            return carry

        lax.fori_loop(0, CHIPS, step, 0)

    @pl.when(sec == 0)
    def _():
        load_hidden(xa.at[0], core * CHIPS, recv_sem.at[S_IN, 0])

    @pl.when(sec != 0)
    def _():
        load_hidden(x0, 0, misc_sem.at[0])

    for w in weight:
        w.start()

    barrier = pltpu.get_barrier_semaphore()

    def greet(k, carry):
        pl.semaphore_signal(
            barrier, inc=1, device_id=(sec, lax.rem(me + k, N)), device_id_type=MESH
        )
        return carry

    lax.fori_loop(1, N, greet, 0)
    for k in range(1, SECTIONS):
        pl.semaphore_signal(
            barrier, inc=1, device_id=(lax.rem(sec + k, SECTIONS), me), device_id_type=MESH
        )

    weight[0].wait()
    weight[1].wait()

    def permute_rows(i, carry):
        rows = pl.ds(pl.multiple_of(i * 512, 512), 512)
        both = jnp.dot(wkb[rows, :], pk[...], preferred_element_type=F32) + jnp.dot(
            wvb[rows, :], pv[...], preferred_element_type=F32
        )
        wqkv[rows, pl.ds(HD, HD)] = both.astype(BF)
        return carry

    lax.fori_loop(0, D // 512, permute_rows, 0)

    pl.semaphore_wait(barrier, N - 1 + SECTIONS - 1)

    @pl.when(sec != 0)
    def _():
        pltpu.make_async_copy(x0, x0, misc_sem.at[0]).wait()
        pltpu.make_async_remote_copy(
            src_ref=x0, dst_ref=xa.at[sec, half(core)], send_sem=misc_sem.at[1],
            recv_sem=recv_sem.at[S_IN, sec], device_id=(0, me), device_id_type=MESH,
        ).start()

    weight[2].wait()

    def gather_send(buf, phase, m):
        view = buf.at[m, mine]
        others(lambda chip_to: remote(view, view, phase, m, sec, chip_to * 2 + core).start())

    def gather_pass(buf, phase, m):
        view = buf.at[m, half(core)]
        remote(view, view, phase, m, sec, partner).start()

    def scaled(buf, m, which, slot, gain):
        total = jnp.zeros((LEN, 128), F32)
        for j in range(CHIPS):
            block = which * CHIPS + j
            value = buf[m, block].astype(F32)
            total = total + value * value
            factor = gain[:, pl.ds(pl.multiple_of(block * 128, 128), 128)].astype(F32)
            xg[slot, :, j * 128 : (j + 1) * 128] = (value * factor).astype(BF)
        return total

    def inverse_rms(total):
        mean_sq = jnp.sum(total, axis=-1, keepdims=True) * (1.0 / D)
        return lax.rsqrt(mean_sq + EPSILON)

    def rows_of(which):
        return pl.ds(pl.multiple_of(which * (D // 2), D // 2), D // 2)

    def arrive(m):
        @pl.when(sec != 0)
        def _():
            received(yb.at[m], S_Y, m)
            gather_send(xa, S_AG1, m)

    def project(m):
        @pl.when(sec == 0)
        def _():
            received(xa.at[m, pl.ds(0, CHIPS)], S_IN, m)

        @pl.when(sec != 0)
        def _():
            received(xa.at[m, pl.ds(0, CHIPS - 1)], S_AG1, m)

        gather_pass(xa, S_PASS1, m)
        total = scaled(xa, m, core, 0, again)
        qkv = jnp.dot(xg[0], wqkv[rows_of(core), :], preferred_element_type=F32)
        received(xa.at[m, pl.ds(0, CHIPS)], S_PASS1, m)
        total = total + scaled(xa, m, rest, 1, again)
        qkv = qkv + jnp.dot(xg[1], wqkv[rows_of(rest), :], preferred_element_type=F32)
        qkv = qkv * inverse_rms(total)
        kv = qkv[:, HD : 2 * HD].astype(BF).astype(F32)
        turned = kv.T
        pairs = jnp.concatenate([turned[0:32, :], turned[32:64, :]], axis=1)
        kvs[m] = pairs.reshape(KV_HEADS, 4, 128)
        kvr[m, me] = kvs[m, kv_id]

        def send(k, carry):
            d = lax.rem(me + k, N)
            remote(
                kvs.at[m, d // (HEADS // KV_HEADS)], kvr.at[m, me], S_KV, m, sec, d
            ).start()
            return carry

        lax.fori_loop(1, N, send, 0)
        q = qkv[:, :HD]
        mid = HD // 2
        swapped = jnp.concatenate([q[:, mid:], q[:, :mid]], axis=1)
        qs[m] = (q * cs[...] + swapped * sn[...]).astype(BF)

    def reduce_send(left, weights, phase, pass_phase, recv, m):
        def term(which, i):
            first = which * (D // 2) + i * 1024
            cols = pl.ds(pl.multiple_of(first, 1024), 1024)
            return jnp.dot(left, weights[:, cols], preferred_element_type=F32)

        def away(i, carry):
            value = term(rest, i).astype(BF)
            for j in range(8):
                pt[phase - S_RS1, m, i * 8 + j] = value[:, j * 128 : (j + 1) * 128]
            return carry

        lax.fori_loop(0, 2, away, 0)
        give = remote(pt.at[phase - S_RS1, m], dr.at[phase - S_RS1, m], pass_phase, m, sec, partner)
        give.start()

        def kept(i, carry):
            value = term(core, i)
            for j in range(8):
                own[i * 8 + j] = value[:, j * 128 : (j + 1) * 128]
            return carry

        lax.fori_loop(0, 2, kept, 0)
        give.wait()

        def add(j, carry):
            ps[phase - S_RS1, m, j] = (own[j] + dr[phase - S_RS1, m, j].astype(F32)).astype(BF)
            return carry

        lax.fori_loop(0, CHIPS, add, 0, unroll=4)
        others(
            lambda chip_to: remote(
                ps.at[phase - S_RS1, m, chip_to], recv.at[m, chip], phase, m, sec,
                chip_to * 2 + core,
            ).start()
        )
        recv[m, chip] = ps[phase - S_RS1, m, chip]

    def summed(recv, phase, m):
        received(recv.at[m, pl.ds(0, CHIPS - 1)], phase, m)
        total = recv[m, 0].astype(F32)
        for j in range(1, CHIPS):
            total = total + recv[m, j].astype(F32)
        return total

    def attend(m):
        received(kvr.at[m, pl.ds(0, N - 1)], S_KV, m)
        both = kvr[m].reshape(HD, 128)
        kt = both[:, :LEN]
        vt = both[:, LEN:].astype(BF)
        mid = HD // 2
        u, v = kt[:mid], kt[mid:]
        keys = jnp.concatenate(
            [u * cst[...] - v * snt[...], u * snt[...] + v * cst[...]], axis=0
        ).astype(BF)
        scores = jnp.dot(qs[m], keys, preferred_element_type=F32) * HD ** (-0.5)
        row = lax.broadcasted_iota(jnp.int32, (LEN, LEN), 0)
        col = lax.broadcasted_iota(jnp.int32, (LEN, LEN), 1)
        scores = jnp.where(row >= col, scores, -jnp.inf)
        top = jnp.max(scores, axis=-1, keepdims=True)
        e = jnp.exp(scores - top)
        prob = (e / jnp.sum(e, axis=-1, keepdims=True)).astype(BF)
        context = lax.dot_general(
            prob, vt, (((1,), (1,)), ((), ())), preferred_element_type=F32
        )
        on = jnp.full((LEN, HD), heads[m, 0], jnp.int32) > me
        context = jnp.where(on, context, 0.0).astype(BF)
        reduce_send(context, wob, S_RS1, S_GIVE1, r1, m)

    def attended(m):
        value = xa[m, mine].astype(F32) + summed(r1, S_RS1, m)
        att[m] = value
        xb[m, mine] = value.astype(BF)
        gather_send(xb, S_AG2, m)

    def feed(m):
        received(xb.at[m, pl.ds(0, CHIPS - 1)], S_AG2, m)
        gather_pass(xb, S_PASS2, m)
        total = scaled(xb, m, core, 0, fgain)

        def first(i, carry):
            cols = pl.ds(pl.multiple_of(i * 256, 256), 256)
            acc[0, :, cols] = jnp.dot(
                xg[0], wgb[rows_of(core), cols], preferred_element_type=F32
            )
            acc[1, :, cols] = jnp.dot(
                xg[0], wub[rows_of(core), cols], preferred_element_type=F32
            )
            return carry

        lax.fori_loop(0, 2, first, 0)
        received(xb.at[m, pl.ds(0, CHIPS)], S_PASS2, m)
        scale = inverse_rms(total + scaled(xb, m, rest, 1, fgain))
        limit = jnp.full((LEN, 256), blocks[m, 0], jnp.int32) * BLOCK

        def second(i, carry):
            cols = pl.ds(pl.multiple_of(i * 256, 256), 256)
            gate = acc[0, :, cols] + jnp.dot(
                xg[1], wgb[rows_of(rest), cols], preferred_element_type=F32
            )
            up = acc[1, :, cols] + jnp.dot(
                xg[1], wub[rows_of(rest), cols], preferred_element_type=F32
            )
            gate, up = gate * scale, up * scale
            ids = me * UNITS + i * 256 + lax.broadcasted_iota(jnp.int32, (LEN, 256), 1)
            value = gate / (1.0 + jnp.exp(-gate)) * up
            hbuf[:, cols] = jnp.where(ids < limit, value, 0.0).astype(BF)
            return carry

        lax.fori_loop(0, 2, second, 0)
        reduce_send(hbuf[...], wdb, S_RS2, S_GIVE2, r2, m)

    def finish(m):
        yb[m] = (att[m] + summed(r2, S_RS2, m)).astype(BF)

        @pl.when(sec < SECTIONS - 1)
        def _():
            remote(yb.at[m], xa.at[m, mine], S_Y, m, sec + 1, me).start()

        @pl.when((sec == SECTIONS - 1) & (m < MICRO - 1))
        def _():
            pltpu.make_async_remote_copy(
                src_ref=yb.at[m], dst_ref=obuf.at[0, mine], send_sem=send_sem.at[S_Y, m],
                recv_sem=misc_sem.at[2], device_id=(m, me), device_id_type=MESH,
            ).start()

    def slot(i, carry):
        @pl.when(i < MICRO)
        def _():
            arrive(i)
            project(i)

        @pl.when(i == 0)
        def _():
            weight[3].wait()

        @pl.when(i == 1)
        def _():
            for w in weight[4:]:
                w.wait()

        @pl.when(i > 0)
        def _():
            feed(i - 1)

        @pl.when(i < MICRO)
        def _():
            attend(i)

        @pl.when(i > 0)
        def _():
            finish(i - 1)

        @pl.when(i < MICRO)
        def _():
            attended(i)

        return carry

    lax.fori_loop(0, MICRO + 1, slot, 0)

    @pl.when(sec == SECTIONS - 1)
    def _():
        obuf[0, mine] = yb[MICRO - 1]

    @pl.when(sec != SECTIONS - 1)
    def _():
        pltpu.make_async_copy(yb.at[0], yb.at[0], misc_sem.at[2]).wait()

    gather_send(obuf, S_AG3, 0)
    received(obuf.at[0, pl.ds(0, CHIPS - 1)], S_AG3, 0)
    gather_pass(obuf, S_PASS3, 0)
    near = pltpu.make_async_copy(
        obuf.at[0, half(core)], out.at[half(core)], misc_sem.at[3]
    )
    near.start()

    def drain(m, carry):
        @pl.when(sec != 0)
        def _():
            sent(xa.at[m, pl.ds(0, CHIPS - 1)], S_AG1, m)

        sent(xa.at[m, pl.ds(0, CHIPS)], S_PASS1, m)
        sent(kvr.at[m, pl.ds(0, N - 1)], S_KV, m)
        sent(r1.at[m, pl.ds(0, CHIPS - 1)], S_RS1, m)
        sent(xb.at[m, pl.ds(0, CHIPS - 1)], S_AG2, m)
        sent(xb.at[m, pl.ds(0, CHIPS)], S_PASS2, m)
        sent(r2.at[m, pl.ds(0, CHIPS - 1)], S_RS2, m)

        @pl.when((sec < SECTIONS - 1) | (m < MICRO - 1))
        def _():
            sent(yb.at[m], S_Y, m)

        return carry

    lax.fori_loop(0, MICRO, drain, 0)

    @pl.when(sec != 0)
    def _():
        pltpu.make_async_copy(x0, x0, misc_sem.at[1]).wait()

    sent(obuf.at[0, pl.ds(0, CHIPS - 1)], S_AG3, 0)
    received(obuf.at[0, pl.ds(0, CHIPS)], S_PASS3, 0)
    far = pltpu.make_async_copy(obuf.at[0, half(rest)], out.at[half(rest)], misc_sem.at[4])
    far.start()
    sent(obuf.at[0, pl.ds(0, CHIPS)], S_PASS3, 0)
    near.wait()
    far.wait()


def tables():
    half = HD // 2
    frequency = ROPE_BASE ** (-(np.arange(half, dtype=np.float64) / half))
    angles = np.arange(LEN, dtype=np.float64)[:, None] * frequency[None, :]
    c, s = np.cos(angles).astype(np.float32), np.sin(angles).astype(np.float32)
    cs = np.concatenate([c, c], axis=1)
    sn = np.concatenate([-s, s], axis=1)
    pk = np.zeros((32, HD), np.float32)
    pv = np.zeros((32, HD), np.float32)
    for j in range(4):
        for k in range(KV_HEADS):
            pk[j * KV_HEADS + k, k * 4 + j] = 1.0
            pv[j * KV_HEADS + k, 32 + k * 4 + j] = 1.0
    return (
        jnp.asarray(cs), jnp.asarray(sn),
        jnp.asarray(np.ascontiguousarray(c.T)), jnp.asarray(np.ascontiguousarray(s.T)),
        jnp.asarray(pk, BF), jnp.asarray(pv, BF),
    )


def per_device(*args):
    any_spec = pl.BlockSpec(memory_space=pl.ANY)
    vmem = pl.BlockSpec(memory_space=pltpu.VMEM)
    smem = pl.BlockSpec(memory_space=pltpu.SMEM)
    piece = (LEN, 128)
    gathered = pl.pallas_call(
        body,
        out_shape=jax.ShapeDtypeStruct((N, *piece), BF),
        in_specs=[
            any_spec, vmem, any_spec, any_spec, any_spec, any_spec, vmem, any_spec, any_spec,
            any_spec, smem, smem, vmem, vmem, vmem, vmem, vmem, vmem,
        ],
        out_specs=any_spec,
        scratch_shapes=[
            pltpu.VMEM((CHIPS, *piece), BF),
            pltpu.VMEM((MICRO, N, *piece), BF),
            pltpu.VMEM((MICRO, N, *piece), BF),
            pltpu.VMEM((MICRO, CHIPS, *piece), BF),
            pltpu.VMEM((MICRO, CHIPS, *piece), BF),
            pltpu.VMEM((2, MICRO, CHIPS, *piece), BF),
            pltpu.VMEM((2, MICRO, CHIPS, *piece), BF),
            pltpu.VMEM((2, MICRO, CHIPS, *piece), BF),
            pltpu.VMEM((CHIPS, *piece), F32),
            pltpu.VMEM((MICRO, KV_HEADS, 4, 128), F32),
            pltpu.VMEM((MICRO, N, 4, 128), F32),
            pltpu.VMEM((1, N, *piece), BF),
            pltpu.VMEM((MICRO, *piece), BF),
            pltpu.VMEM((MICRO, *piece), F32),
            pltpu.VMEM((2, LEN, D // 2), BF),
            pltpu.VMEM((2, LEN, UNITS), F32),
            pltpu.VMEM((LEN, UNITS), BF),
            pltpu.VMEM((MICRO, *piece), BF),
            pltpu.VMEM((D, 256), BF),
            pltpu.VMEM((D, 32), BF),
            pltpu.VMEM((D, 32), BF),
            pltpu.VMEM((HD, D), BF),
            pltpu.VMEM((D, UNITS), BF),
            pltpu.VMEM((D, UNITS), BF),
            pltpu.VMEM((UNITS, D), BF),
            pltpu.SemaphoreType.DMA((13, MICRO)),
            pltpu.SemaphoreType.DMA((13, MICRO)),
            pltpu.SemaphoreType.DMA((5,)),
            pltpu.SemaphoreType.DMA((7,)),
        ],
        compiler_params=pltpu.CompilerParams(
            collective_id=0, has_side_effects=True, vmem_limit_bytes=56 * 1024 * 1024
        ),
    )(*args, *tables())
    return gathered.transpose(1, 0, 2).reshape(1, 1, LEN, D)


def solution(mesh):
    return jax.shard_map(
        per_device,
        mesh=mesh,
        in_specs=(
            P(None, "section", None, None),
            P("section", None),
            P("section", None, "mp"),
            P("section", None, "mp"),
            P("section", None, "mp"),
            P("section", "mp", None),
            P("section", None),
            P("section", None, "mp"),
            P("section", None, "mp"),
            P("section", "mp", None),
            P(None, "section"),
            P(None, "section"),
        ),
        out_specs=P(None, "section", None, None),
        check_vma=False,
    )
```

time: 349 us -> 259 us (0.74)
  Pallas kernels: 339 us -> 249 us
    pallas_call x1, Pallas kernels: 339 us -> 249 us  [per_device(): pl.pallas_call(body, out_shape=jax.ShapeDtypeStruct((N, *piece), BF), in_...]
where the time goes in v2:
time: 259 us; the launch traced here: 258 us
  Pallas kernels  249 us (96%)
  local copies, waits for them, and re-layouts  9.64 us (4%)
    pallas_call x1, Pallas kernels, per_device(): pl.pallas_call(body, out_shape=jax.ShapeDtypeStruct((N, *piece), BF), in_...  249 us
    unnamed x4, local copies, waits for them, and re-layouts  7.23 us

profile of v2, /device:TPU:25, one launch (start us, length us, event | category | flops | bytes accessed | tf_op | source)
XLA Modules:
  0.0 258.3 jit_solution(9013836560669388164)
XLA Ops:
  0.0 1.3 copy.25.blocks
  1.3 1.3 copy.26.heads
  2.6 2.3 copy.23.wk
  4.9 2.3 copy.24.wv
  7.2 248.7 %shard_map.172 = bf16[32,64,128]{2,1,0:T(8,128)(2,1)} custom-call(bf16[1,1,64,4096]{3,2,1,0:T(8,128)(2,1)} %hid.1, bf16[1,4096]{1,0:T(2,128)(2,1)} %again.1, bf16[1,4096,128]{2,1,0:T(8,128)(2,1)} %wq.1, bf16[1,4096,32]{2,1,0:T(8,128)(2,1)} %copy.23.wk, bf16[1,4096,32]{2,1,0:T(8,128)(2,1)} %copy.24.wv, bf16[1,128,4096]{2,1,0:T(8,128)(2,1)} %wo.1, ...), custom_call_target="tpu_custom_call" | custom-call | tf_op jit(solution)/shard_map/pallas_call | solution.py:444
  255.9 1.4 copy.27
  257.3 1.0 reshape.3

commit v3 on v2

--- a/solution.py
+++ b/solution.py
@@ -26,7 +26,8 @@
 CHIPS = 16
 (
     S_IN, S_Y, S_AG1, S_PASS1, S_KV, S_GIVE1, S_RS1, S_RS2, S_AG2, S_PASS2, S_GIVE2, S_AG3, S_PASS3,
-) = range(13)
+    S_W,
+) = range(14)
 RING = (0, 1, 2, 1)
 FAR_FIRST = sorted(
     [(dx, dz) for dx in range(4) for dz in range(4) if (dx, dz) != (0, 0)],
@@ -36,10 +37,10 @@
 
 def body(
     hid, again, wq, wk, wv, wo, fgain, wg, wu, wd, blocks, heads,
-    cs, sn, cst, snt, pk, pv,
+    cs, sn, pk, pv, tk, tv, order,
     out,
     x0, xa, xb, r1, r2, pt, ps, dr, own, kvs, kvr, obuf, yb, att, xg, acc, hbuf, qs,
-    wqkv, wkb, wvb, wob, wgb, wub, wdb,
+    ks, vs, aq, wgive, wtake, wqkv, wkb, wvb, wob, wgb, wub, wdb,
     send_sem, recv_sem, misc_sem, w_sem,
 ):
     sec = lax.axis_index("section")
@@ -117,6 +118,7 @@
 
     weight[0].wait()
     weight[1].wait()
+    nt = (((1,), (1,)), ((), ()))
 
     def permute_rows(i, carry):
         rows = pl.ds(pl.multiple_of(i * 512, 512), 512)
@@ -126,7 +128,21 @@
         wqkv[rows, pl.ds(HD, HD)] = both.astype(BF)
         return carry
 
-    lax.fori_loop(0, D // 512, permute_rows, 0)
+    def turn_rows(i, carry):
+        rows = pl.ds(pl.multiple_of(i * 512, 512), 512)
+        both = lax.dot_general(
+            tk[...], wkb[rows, :], nt, preferred_element_type=F32
+        ) + lax.dot_general(tv[...], wvb[rows, :], nt, preferred_element_type=F32)
+        wgive[:, :, rows] = both.reshape(KV_HEADS, 8, 512).astype(BF)
+        return carry
+
+    @pl.when(sec == 0)
+    def _():
+        lax.fori_loop(0, D // 512, permute_rows, 0)
+
+    @pl.when(sec != 0)
+    def _():
+        lax.fori_loop(0, D // 512, turn_rows, 0)
 
     pl.semaphore_wait(barrier, N - 1 + SECTIONS - 1)
 
@@ -137,6 +153,28 @@
             src_ref=x0, dst_ref=xa.at[sec, half(core)], send_sem=misc_sem.at[1],
             recv_sem=recv_sem.at[S_IN, sec], device_id=(0, me), device_id_type=MESH,
         ).start()
+        others(
+            lambda chip_to: remote(
+                wgive.at[chip_to // 2], wtake.at[mine], S_W, 0, sec, chip_to * 2 + core
+            ).start()
+        )
+        wtake[mine] = wgive[chip // 2]
+        received(wtake.at[pl.ds(0, CHIPS - 1)], S_W, 0)
+        view = wtake.at[half(core)]
+        swap = remote(view, view, S_W, 1, sec, partner)
+        swap.start()
+        swap.wait()
+
+        def put_in_order(i, carry):
+            rows = pl.ds(pl.multiple_of(i * 512, 512), 512)
+            chunk = wtake[:, :, rows].astype(F32).reshape(2 * HD, 512).T.astype(BF)
+            wqkv[rows, pl.ds(HD, 2 * HD)] = jnp.dot(
+                chunk, order[...], preferred_element_type=F32
+            ).astype(BF)
+            return carry
+
+        lax.fori_loop(0, D // 512, put_in_order, 0)
+        sent(wtake.at[pl.ds(0, CHIPS - 1)], S_W, 0)
 
     weight[2].wait()
 
@@ -182,29 +220,48 @@
 
         gather_pass(xa, S_PASS1, m)
         total = scaled(xa, m, core, 0, again)
-        qkv = jnp.dot(xg[0], wqkv[rows_of(core), :], preferred_element_type=F32)
+        front, back = pl.ds(0, 2 * HD), pl.ds(2 * HD, HD)
+        aq[:, front] = jnp.dot(xg[0], wqkv[rows_of(core), front], preferred_element_type=F32)
+
+        @pl.when(sec != 0)
+        def _():
+            aq[:, back] = jnp.dot(xg[0], wqkv[rows_of(core), back], preferred_element_type=F32)
+
         received(xa.at[m, pl.ds(0, CHIPS)], S_PASS1, m)
         total = total + scaled(xa, m, rest, 1, again)
-        qkv = qkv + jnp.dot(xg[1], wqkv[rows_of(rest), :], preferred_element_type=F32)
-        qkv = qkv * inverse_rms(total)
-        kv = qkv[:, HD : 2 * HD].astype(BF).astype(F32)
-        turned = kv.T
-        pairs = jnp.concatenate([turned[0:32, :], turned[32:64, :]], axis=1)
-        kvs[m] = pairs.reshape(KV_HEADS, 4, 128)
-        kvr[m, me] = kvs[m, kv_id]
-
-        def send(k, carry):
-            d = lax.rem(me + k, N)
-            remote(
-                kvs.at[m, d // (HEADS // KV_HEADS)], kvr.at[m, me], S_KV, m, sec, d
-            ).start()
-            return carry
-
-        lax.fori_loop(1, N, send, 0)
-        q = qkv[:, :HD]
+        scale = inverse_rms(total)
+        qk = aq[:, front] + jnp.dot(xg[1], wqkv[rows_of(rest), front], preferred_element_type=F32)
+        qk = qk * scale
+        qs[m] = rotated(qk[:, :HD])
+
+        @pl.when(sec != 0)
+        def _():
+            ks[m] = rotated(qk[:, HD:].astype(BF).astype(F32))
+            v = aq[:, back] + jnp.dot(
+                xg[1], wqkv[rows_of(rest), back], preferred_element_type=F32
+            )
+            vs[m] = (v * scale).astype(BF)
+
+        @pl.when(sec == 0)
+        def _():
+            turned = qk[:, HD:].astype(BF).astype(F32).T
+            pairs = jnp.concatenate([turned[0:32, :], turned[32:64, :]], axis=1)
+            kvs[m] = pairs.reshape(KV_HEADS, 4, 128)
+            kvr[m, me] = kvs[m, kv_id]
+
+            def send(k, carry):
+                d = lax.rem(me + k, N)
+                remote(
+                    kvs.at[m, d // (HEADS // KV_HEADS)], kvr.at[m, me], S_KV, m, sec, d
+                ).start()
+                return carry
+
+            lax.fori_loop(1, N, send, 0)
+
+    def rotated(value):
         mid = HD // 2
-        swapped = jnp.concatenate([q[:, mid:], q[:, :mid]], axis=1)
-        qs[m] = (q * cs[...] + swapped * sn[...]).astype(BF)
+        swapped = jnp.concatenate([value[:, mid:], value[:, :mid]], axis=1)
+        return (value * cs[...] + swapped * sn[...]).astype(BF)
 
     def reduce_send(left, weights, phase, pass_phase, recv, m):
         def term(which, i):
@@ -252,25 +309,21 @@
         return total
 
     def attend(m):
-        received(kvr.at[m, pl.ds(0, N - 1)], S_KV, m)
-        both = kvr[m].reshape(HD, 128)
-        kt = both[:, :LEN]
-        vt = both[:, LEN:].astype(BF)
-        mid = HD // 2
-        u, v = kt[:mid], kt[mid:]
-        keys = jnp.concatenate(
-            [u * cst[...] - v * snt[...], u * snt[...] + v * cst[...]], axis=0
-        ).astype(BF)
-        scores = jnp.dot(qs[m], keys, preferred_element_type=F32) * HD ** (-0.5)
+        @pl.when(sec == 0)
+        def _():
+            received(kvr.at[m, pl.ds(0, N - 1)], S_KV, m)
+            both = kvr[m].reshape(HD, 128).T
+            ks[m] = rotated(both[:LEN])
+            vs[m] = both[LEN:].astype(BF)
+
+        scores = lax.dot_general(qs[m], ks[m], nt, preferred_element_type=F32) * HD ** (-0.5)
         row = lax.broadcasted_iota(jnp.int32, (LEN, LEN), 0)
         col = lax.broadcasted_iota(jnp.int32, (LEN, LEN), 1)
         scores = jnp.where(row >= col, scores, -jnp.inf)
         top = jnp.max(scores, axis=-1, keepdims=True)
         e = jnp.exp(scores - top)
         prob = (e / jnp.sum(e, axis=-1, keepdims=True)).astype(BF)
-        context = lax.dot_general(
-            prob, vt, (((1,), (1,)), ((), ())), preferred_element_type=F32
-        )
+        context = jnp.dot(prob, vs[m], preferred_element_type=F32)
         on = jnp.full((LEN, HD), heads[m, 0], jnp.int32) > me
         context = jnp.where(on, context, 0.0).astype(BF)
         reduce_send(context, wob, S_RS1, S_GIVE1, r1, m)
@@ -336,6 +389,9 @@
         @pl.when(i < MICRO)
         def _():
             arrive(i)
+
+        @pl.when((i < MICRO) & (sec == 0))
+        def _():
             project(i)
 
         @pl.when(i == 0)
@@ -350,6 +406,10 @@
         @pl.when(i > 0)
         def _():
             feed(i - 1)
+
+        @pl.when((i < MICRO) & (sec != 0))
+        def _():
+            project(i)
 
         @pl.when(i < MICRO)
         def _():
@@ -389,7 +449,11 @@
             sent(xa.at[m, pl.ds(0, CHIPS - 1)], S_AG1, m)
 
         sent(xa.at[m, pl.ds(0, CHIPS)], S_PASS1, m)
-        sent(kvr.at[m, pl.ds(0, N - 1)], S_KV, m)
+
+        @pl.when(sec == 0)
+        def _():
+            sent(kvr.at[m, pl.ds(0, N - 1)], S_KV, m)
+
         sent(r1.at[m, pl.ds(0, CHIPS - 1)], S_RS1, m)
         sent(xb.at[m, pl.ds(0, CHIPS - 1)], S_AG2, m)
         sent(xb.at[m, pl.ds(0, CHIPS)], S_PASS2, m)
@@ -425,14 +489,23 @@
     sn = np.concatenate([-s, s], axis=1)
     pk = np.zeros((32, HD), np.float32)
     pv = np.zeros((32, HD), np.float32)
+    tk = np.zeros((64, 32), np.float32)
+    tv = np.zeros((64, 32), np.float32)
     for j in range(4):
         for k in range(KV_HEADS):
             pk[j * KV_HEADS + k, k * 4 + j] = 1.0
             pv[j * KV_HEADS + k, 32 + k * 4 + j] = 1.0
-    return (
-        jnp.asarray(cs), jnp.asarray(sn),
-        jnp.asarray(np.ascontiguousarray(c.T)), jnp.asarray(np.ascontiguousarray(s.T)),
-        jnp.asarray(pk, BF), jnp.asarray(pv, BF),
+            tk[k * 8 + j, j * KV_HEADS + k] = 1.0
+            tv[k * 8 + 4 + j, j * KV_HEADS + k] = 1.0
+    order = np.zeros((2 * HD, 2 * HD), np.float32)
+    for c in range(2):
+        for q in range(CHIPS):
+            for r in range(4):
+                row, col = (c * CHIPS + q) * 8 + r, 4 * (2 * q + c) + r
+                order[row, col] = 1.0
+                order[row + 4, HD + col] = 1.0
+    return (jnp.asarray(cs), jnp.asarray(sn)) + tuple(
+        jnp.asarray(a, BF) for a in (pk, pv, tk, tv, order)
     )
 
 
@@ -446,7 +519,7 @@
         out_shape=jax.ShapeDtypeStruct((N, *piece), BF),
         in_specs=[
             any_spec, vmem, any_spec, any_spec, any_spec, any_spec, vmem, any_spec, any_spec,
-            any_spec, smem, smem, vmem, vmem, vmem, vmem, vmem, vmem,
+            any_spec, smem, smem, vmem, vmem, vmem, vmem, vmem, vmem, vmem,
         ],
         out_specs=any_spec,
         scratch_shapes=[
@@ -468,15 +541,20 @@
             pltpu.VMEM((2, LEN, UNITS), F32),
             pltpu.VMEM((LEN, UNITS), BF),
             pltpu.VMEM((MICRO, *piece), BF),
-            pltpu.VMEM((D, 256), BF),
+            pltpu.VMEM((MICRO, *piece), BF),
+            pltpu.VMEM((MICRO, *piece), BF),
+            pltpu.VMEM((LEN, 3 * HD), F32),
+            pltpu.VMEM((KV_HEADS, 8, D), BF),
+            pltpu.VMEM((N, 8, D), BF),
+            pltpu.VMEM((D, 3 * HD), BF),
             pltpu.VMEM((D, 32), BF),
             pltpu.VMEM((D, 32), BF),
             pltpu.VMEM((HD, D), BF),
             pltpu.VMEM((D, UNITS), BF),
             pltpu.VMEM((D, UNITS), BF),
             pltpu.VMEM((UNITS, D), BF),
-            pltpu.SemaphoreType.DMA((13, MICRO)),
-            pltpu.SemaphoreType.DMA((13, MICRO)),
+            pltpu.SemaphoreType.DMA((14, MICRO)),
+            pltpu.SemaphoreType.DMA((14, MICRO)),
             pltpu.SemaphoreType.DMA((5,)),
             pltpu.SemaphoreType.DMA((7,)),
         ],

time: 259 us -> 221 us (0.85)
  Pallas kernels: 249 us -> 211 us
    pallas_call x1, Pallas kernels: 249 us -> 211 us  [per_device(): pl.pallas_call(body, out_shape=jax.ShapeDtypeStruct((N, *piece), BF), in_...]
where the time goes in v3:
time: 221 us
  Pallas kernels  211 us (95%)
  local copies, waits for them, and re-layouts  9.64 us (4%)
    pallas_call x1, Pallas kernels, per_device(): pl.pallas_call(body, out_shape=jax.ShapeDtypeStruct((N, *piece), BF), in_...  211 us
    unnamed x4, local copies, waits for them, and re-layouts  7.23 us

profile of v3, /device:TPU:25, one launch (start us, length us, event | category | flops | bytes accessed | tf_op | source)
XLA Modules:
  0.0 221.0 jit_solution(16353321152630759941)
XLA Ops:
  0.0 1.3 copy.26.blocks
  1.3 1.3 copy.27.heads
  2.6 2.3 %copy.24.wk = bf16[1,4096,32]{2,1,0:T(8,128)(2,1)} copy(bf16[1,4096,32]{1,2,0:T(8,128)(2,1)} %param.22) | data formatting | bytes 524288 | tf_op args[3]
  4.9 2.3 %copy.25.wv = bf16[1,4096,32]{2,1,0:T(8,128)(2,1)} copy(bf16[1,4096,32]{1,2,0:T(8,128)(2,1)} %param.23) | data formatting | bytes 524288 | tf_op args[4]
  7.2 211.3 %shard_map.181 = bf16[32,64,128]{2,1,0:T(8,128)(2,1)} custom-call(bf16[1,1,64,4096]{3,2,1,0:T(8,128)(2,1)} %hid.1, bf16[1,4096]{1,0:T(2,128)(2,1)} %again.1, bf16[1,4096,128]{2,1,0:T(8,128)(2,1)} %wq.1, bf16[1,4096,32]{2,1,0:T(8,128)(2,1)} %copy.24.wk, bf16[1,4096,32]{2,1,0:T(8,128)(2,1)} %copy.25.wv, bf16[1,128,4096]{2,1,0:T(8,128)(2,1)} %wo.1, ...), custom_call_target="tpu_custom_call" | custom-call | tf_op jit(solution)/shard_map/pallas_call | solution.py:517
  218.5 1.4 copy.28
  219.9 1.0 reshape.3

commit v4 on v3

--- a/solution.py
+++ b/solution.py
@@ -28,6 +28,26 @@
     S_IN, S_Y, S_AG1, S_PASS1, S_KV, S_GIVE1, S_RS1, S_RS2, S_AG2, S_PASS2, S_GIVE2, S_AG3, S_PASS3,
     S_W,
 ) = range(14)
+ORDERS = (
+    "P0P1T0P2T1C0T2P3C1D0C2D1E0T3D2E1C3E2D3E3",
+    "A0P0A1T0A2P1T1C0P2T2C1A3D0C2D1P3E0T3D2E1C3E2D3E3",
+    "A0P0A1T0A2P1T1C0P2T2A3C1D0C2P3T3D1E0C3D2E1D3E2E3",
+    "A0A1P0T0P1A2T1A3C0P2T2C1P3T3C2D0C3D1D2D3E0E1E2E3",
+)
+STEPS, PACK = 24, 6
+
+
+def packed(order):
+    codes = ["APTCDE".index(a) * MICRO + int(b) for a, b in zip(order[::2], order[1::2])]
+    codes += [SKIP] * (STEPS - len(codes))
+    return [
+        sum(c << (5 * i) for i, c in enumerate(codes[k : k + PACK]))
+        for k in range(0, STEPS, PACK)
+    ]
+
+
+SKIP = 24
+WORDS = [packed(order) for order in ORDERS]
 RING = (0, 1, 2, 1)
 FAR_FIRST = sorted(
     [(dx, dz) for dx in range(4) for dz in range(4) if (dx, dz) != (0, 0)],
@@ -385,47 +405,33 @@
                 recv_sem=misc_sem.at[2], device_id=(m, me), device_id_type=MESH,
             ).start()
 
-    def slot(i, carry):
-        @pl.when(i < MICRO)
-        def _():
-            arrive(i)
-
-        @pl.when((i < MICRO) & (sec == 0))
-        def _():
-            project(i)
-
-        @pl.when(i == 0)
-        def _():
-            weight[3].wait()
-
-        @pl.when(i == 1)
-        def _():
-            for w in weight[4:]:
-                w.wait()
-
-        @pl.when(i > 0)
-        def _():
-            feed(i - 1)
-
-        @pl.when((i < MICRO) & (sec != 0))
-        def _():
-            project(i)
-
-        @pl.when(i < MICRO)
-        def _():
-            attend(i)
-
-        @pl.when(i > 0)
-        def _():
-            finish(i - 1)
-
-        @pl.when(i < MICRO)
-        def _():
-            attended(i)
+    work = (arrive, project, attend, attended, feed, finish)
+    waits = {2: weight[3:4], 4: weight[4:]}
+
+    def step(t, carry):
+        word = jnp.int32(0)
+        for s in range(SECTIONS):
+            for k in range(STEPS // PACK):
+                here = (sec == s) & (t // PACK == k)
+                word = jnp.where(here, jnp.int32(WORDS[s][k]), word)
+        for k in range(PACK - 1):
+            word = jnp.where(lax.rem(t, PACK) > k, word // 32, word)
+        code = lax.rem(word, 32)
+        kind, m = code // MICRO, lax.rem(code, MICRO)
+        for i, fn in enumerate(work):
+            @pl.when(kind == i)
+            def _():
+                if i in waits:
+                    @pl.when(m == 0)
+                    def _():
+                        for w in waits[i]:
+                            w.wait()
+
+                fn(m)
 
         return carry
 
-    lax.fori_loop(0, MICRO + 1, slot, 0)
+    lax.fori_loop(0, STEPS, step, 0)
 
     @pl.when(sec == SECTIONS - 1)
     def _():

time: 221 us -> 210 us (0.950)
  Pallas kernels: 211 us -> 200 us
    pallas_call x1, Pallas kernels: 211 us -> 200 us  [per_device(): pl.pallas_call(body, out_shape=jax.ShapeDtypeStruct((N, *piece), BF), in_...]
where the time goes in v4:
time: 210 us
  Pallas kernels  200 us (95%)
  local copies, waits for them, and re-layouts  9.64 us (5%)
    pallas_call x1, Pallas kernels, per_device(): pl.pallas_call(body, out_shape=jax.ShapeDtypeStruct((N, *piece), BF), in_...  200 us
    unnamed x4, local copies, waits for them, and re-layouts  7.23 us

profile of v4, /device:TPU:25, one launch (start us, length us, event | category | flops | bytes accessed | tf_op | source)
XLA Modules:
  0.0 210.0 jit_solution(1942017843095671459)
XLA Ops:
  0.0 1.3 copy.26.blocks
  1.3 1.3 copy.27.heads
  2.6 2.3 %copy.24.wk = bf16[1,4096,32]{2,1,0:T(8,128)(2,1)} copy(bf16[1,4096,32]{1,2,0:T(8,128)(2,1)} %param.22) | data formatting | bytes 524288 | tf_op args[3]
  4.9 2.3 %copy.25.wv = bf16[1,4096,32]{2,1,0:T(8,128)(2,1)} copy(bf16[1,4096,32]{1,2,0:T(8,128)(2,1)} %param.23) | data formatting | bytes 524288 | tf_op args[4]
  7.2 200.4 %shard_map.181 = bf16[32,64,128]{2,1,0:T(8,128)(2,1)} custom-call(bf16[1,1,64,4096]{3,2,1,0:T(8,128)(2,1)} %hid.1, bf16[1,4096]{1,0:T(2,128)(2,1)} %again.1, bf16[1,4096,128]{2,1,0:T(8,128)(2,1)} %wq.1, bf16[1,4096,32]{2,1,0:T(8,128)(2,1)} %copy.24.wk, bf16[1,4096,32]{2,1,0:T(8,128)(2,1)} %copy.25.wv, bf16[1,128,4096]{2,1,0:T(8,128)(2,1)} %wo.1, ...), custom_call_target="tpu_custom_call" | custom-call | tf_op jit(solution)/shard_map/pallas_call | solution.py:523
  207.6 1.4 copy.28
  209.0 1.0 reshape.3

commit v5 on v4

--- a/solution.py
+++ b/solution.py
@@ -295,7 +295,7 @@
                 pt[phase - S_RS1, m, i * 8 + j] = value[:, j * 128 : (j + 1) * 128]
             return carry
 
-        lax.fori_loop(0, 2, away, 0)
+        lax.fori_loop(0, 2, away, 0, unroll=True)
         give = remote(pt.at[phase - S_RS1, m], dr.at[phase - S_RS1, m], pass_phase, m, sec, partner)
         give.start()
 
@@ -305,14 +305,14 @@
                 own[i * 8 + j] = value[:, j * 128 : (j + 1) * 128]
             return carry
 
-        lax.fori_loop(0, 2, kept, 0)
+        lax.fori_loop(0, 2, kept, 0, unroll=True)
         give.wait()
 
         def add(j, carry):
             ps[phase - S_RS1, m, j] = (own[j] + dr[phase - S_RS1, m, j].astype(F32)).astype(BF)
             return carry
 
-        lax.fori_loop(0, CHIPS, add, 0, unroll=4)
+        lax.fori_loop(0, CHIPS, add, 0, unroll=True)
         others(
             lambda chip_to: remote(
                 ps.at[phase - S_RS1, m, chip_to], recv.at[m, chip], phase, m, sec,
@@ -369,7 +369,7 @@
             )
             return carry
 
-        lax.fori_loop(0, 2, first, 0)
+        lax.fori_loop(0, 2, first, 0, unroll=True)
         received(xb.at[m, pl.ds(0, CHIPS)], S_PASS2, m)
         scale = inverse_rms(total + scaled(xb, m, rest, 1, fgain))
         limit = jnp.full((LEN, 256), blocks[m, 0], jnp.int32) * BLOCK
@@ -388,7 +388,7 @@
             hbuf[:, cols] = jnp.where(ids < limit, value, 0.0).astype(BF)
             return carry
 
-        lax.fori_loop(0, 2, second, 0)
+        lax.fori_loop(0, 2, second, 0, unroll=True)
         reduce_send(hbuf[...], wdb, S_RS2, S_GIVE2, r2, m)
 
     def finish(m):

time: 210 us -> 206 us (0.981)
  Pallas kernels: 200 us -> 196 us
    pallas_call x1, Pallas kernels: 200 us -> 196 us  [per_device(): pl.pallas_call(body, out_shape=jax.ShapeDtypeStruct((N, *piece), BF), in_...]
where the time goes in v5:
time: 206 us; the launch traced here: 205 us
  Pallas kernels  196 us (95%)
  local copies, waits for them, and re-layouts  9.64 us (5%)
    pallas_call x1, Pallas kernels, per_device(): pl.pallas_call(body, out_shape=jax.ShapeDtypeStruct((N, *piece), BF), in_...  196 us
    unnamed x4, local copies, waits for them, and re-layouts  7.23 us

profile of v5, /device:TPU:25, one launch (start us, length us, event | category | flops | bytes accessed | tf_op | source)
XLA Modules:
  0.0 205.3 jit_solution(5438815883770037258)
XLA Ops:
  0.0 1.3 copy.26.blocks
  1.3 1.3 copy.27.heads
  2.6 2.3 %copy.24.wk = bf16[1,4096,32]{2,1,0:T(8,128)(2,1)} copy(bf16[1,4096,32]{1,2,0:T(8,128)(2,1)} %param.22) | data formatting | bytes 524288 | tf_op args[3]
  4.9 2.3 %copy.25.wv = bf16[1,4096,32]{2,1,0:T(8,128)(2,1)} copy(bf16[1,4096,32]{1,2,0:T(8,128)(2,1)} %param.23) | data formatting | bytes 524288 | tf_op args[4]
  7.2 195.6 %shard_map.181 = bf16[32,64,128]{2,1,0:T(8,128)(2,1)} custom-call(bf16[1,1,64,4096]{3,2,1,0:T(8,128)(2,1)} %hid.1, bf16[1,4096]{1,0:T(2,128)(2,1)} %again.1, bf16[1,4096,128]{2,1,0:T(8,128)(2,1)} %wq.1, bf16[1,4096,32]{2,1,0:T(8,128)(2,1)} %copy.24.wk, bf16[1,4096,32]{2,1,0:T(8,128)(2,1)} %copy.25.wv, bf16[1,128,4096]{2,1,0:T(8,128)(2,1)} %wo.1, ...), custom_call_target="tpu_custom_call" | custom-call | tf_op jit(solution)/shard_map/pallas_call | solution.py:523
  202.8 1.4 copy.28
  204.2 1.0 reshape.3
